TPU v7x, 512 devices: a whole 4x8x8 slice. The times are simulated.
512 devices in a mesh: wide: 64 (over z_hi, y, core), narrow: 8 (over x, z_lo).
Axes of the slice: x: 4, y: 8, z: 8 (z_hi: 4, z_lo: 2; z = z_hi * 2 + z_lo), core: 2. Of those that a mesh axis runs over, the one named last changes fastest.
Arguments:
- enc_hidden: bfloat16 [12288, 6144], P('wide', 'narrow'), may hold values from -6 to 6
- enc_gain: float32 [6144], P('narrow'), may hold values from 0.1 to 1.9
- cross_weight: bfloat16 [6144, 256], P('narrow'), may hold values from -0.078125 to 0.078125
- assign: int32 [64], P('wide'), may hold values from 0 to 7
- token_ids: int32 [64, 2, 64], P('wide'), may hold values from 0 to 7999, as said below
- cross_table: bfloat16 [8000, 6144], P('wide', 'narrow'), may hold values from -540 to 540
- self_table: bfloat16 [8000, 6144], P('wide', 'narrow'), may hold values from -540 to 540
- kv_table: bfloat16 [8000, 256], P('wide'), may hold values from -6 to 6
- self_cache: bfloat16 [64, 64, 768, 256], P('wide', 'narrow'), may hold values from -6 to 6
Outputs:
- cross_out: bfloat16 [64, 2, 64, 6144], P('wide', None, None, 'narrow')
- self_out: bfloat16 [64, 2, 64, 6144], P('wide', None, 'narrow')
Inputs may be any that keep to these rules, and one draw needn't show every extreme that they name: `token_ids`: within one group, at most 4 of its 128 ids lie in any one of the 64 ranges of 125 consecutive ids, and some range holds exactly 4 of them.
All inputs are finite; a program needn't handle non-finite values.
Results may differ from a plain program's by a relative error of at most 0.009.
The roundings to bfloat16 on the way count: a program that leaves them out, or rounds other values in their place, can miss the bound.
Values may be sent and summed in bfloat16 or wider, within the bound.
No kernel may reach another device: no remote copies, remote signals or barrier semaphores. Data moves between devices by JAX's collectives and lax.ppermute only.
A program may use at most 64 MiB of HBM per device.

v0:
```python
import jax
import jax.numpy as jnp
from jax import lax
from jax.sharding import PartitionSpec as P

D = 6144
HEADS = 48
HEAD = 128
OWN = 8
ENC_LEN = 1536


EPS = 1e-06


def cut_along(shard, dim, length):
    shape = shard.shape
    pieces = shard.reshape(*shape[:dim], length, shape[dim] // length, *shape[dim + 1 :])
    return jnp.moveaxis(pieces, dim, 0)


def sent_and_summed(shard, axis, dim):
    pieces = cut_along(shard, dim, lax.axis_size(axis))
    arrived = lax.all_to_all(pieces, axis, split_axis=0, concat_axis=0, tiled=True)
    return arrived.sum(axis=0)


def sent_together(arrays, axis, dim, along):
    columns = [a.reshape(*a.shape[:along], -1) for a in arrays]
    both = jnp.concatenate(columns, axis=along)
    whole, at, outs = (sent_and_summed(both, axis, dim), 0, [])
    for a, column in zip(arrays, columns):
        piece = whole[..., at : at + column.shape[along]]
        outs.append(piece.reshape(*piece.shape[:along], *a.shape[along:]))
        at += column.shape[along]
    return tuple(outs)


def copy_for_each(shard, axis):
    length = lax.axis_size(axis)
    return lax.all_to_all(
        jnp.broadcast_to(shard[None], (length, *shard.shape)), axis, 0, 0, tiled=True
    )


def joined_along(pieces, dim):
    shape = list(pieces.shape[1:])
    shape[dim] *= pieces.shape[0]
    return jnp.moveaxis(pieces, 0, dim).reshape(shape)


def gather_directly(shard, axis, dim):
    pieces = copy_for_each(shard, axis)
    return joined_along(pieces, dim)


def in_one_piece(arrays, axis, split_dim, concat_dim, along):
    both = jnp.concatenate(arrays, axis=along)
    whole, at, outs = (
        lax.all_to_all(both, axis, split_axis=split_dim, concat_axis=concat_dim, tiled=True),
        0,
        [],
    )
    for a in arrays:
        outs.append(lax.slice_in_dim(whole, at, at + a.shape[along], axis=along))
        at += a.shape[along]
    return tuple(outs)


def body(
    enc_hidden,
    enc_gain,
    cross_weight,
    assign,
    token_ids,
    cross_table,
    self_table,
    kv_table,
    self_cache,
):
    hidden = enc_hidden.astype(jnp.float32)
    part_squares = jnp.sum(hidden * hidden, axis=1)
    scaled = (hidden * enc_gain).astype(jnp.bfloat16)
    part_proj = jnp.dot(scaled, cross_weight, preferred_element_type=jnp.float32)
    problem = assign[0]
    narrow_count = lax.axis_size("narrow")
    narrow_index = lax.axis_index("narrow")
    heads_dev = HEADS // narrow_count
    factor = HEAD ** (-0.5)
    projected, squares = sent_together((part_proj, part_squares), "narrow", 0, 1)
    enc_kv = (projected * lax.rsqrt(squares / D + EPS)[:, None]).astype(jnp.bfloat16)
    gathered = gather_directly(enc_kv, "wide", 0)
    span = ENC_LEN // narrow_count
    mine = lax.dynamic_slice_in_dim(gathered, problem * span, span, 0)
    mine = mine.reshape(OWN, span // OWN, 2 * HEAD)
    problem_kv = gather_directly(mine, "narrow", 1).reshape(ENC_LEN, 2 * HEAD)
    keys = problem_kv[:, :HEAD]
    values = problem_kv[:, HEAD:]
    wide_count = lax.axis_size("wide")
    per_owner = cross_table.shape[0]
    steps = token_ids.shape[1]
    cand = token_ids.shape[2]
    capacity = max(2, 2 * steps * cand // wide_count)
    flat = token_ids.reshape(-1)
    owner = flat // per_owner
    local = flat - owner * per_owner
    owner_hits = (owner[:, None] == jnp.arange(wide_count, dtype=jnp.int32)[None, :]).astype(
        jnp.int32
    )
    earlier = jnp.cumsum(owner_hits, axis=0) - owner_hits
    rank = jnp.sum(earlier * owner_hits, axis=1)
    target = owner * capacity + rank
    slot_match = target[None, :] == jnp.arange(wide_count * capacity, dtype=jnp.int32)[:, None]
    filled = jnp.any(slot_match, axis=1)
    request = jnp.where(filled, jnp.sum(jnp.where(slot_match, local[None, :], 0), axis=1), -1)
    asked = lax.all_to_all(
        request.reshape(wide_count, capacity), "wide", split_axis=0, concat_axis=0, tiled=True
    ).reshape(-1)
    valid = asked >= 0
    index = jnp.where(valid, asked, 0)

    def lookup(table):
        rows = jnp.take(table, index, axis=0)
        rows = jnp.where(valid[:, None], rows, jnp.zeros((), table.dtype))
        return rows.reshape(wide_count, capacity, table.shape[1])

    returned = in_one_piece(
        (lookup(cross_table), lookup(self_table), lookup(kv_table)), "wide", 0, 0, 2
    )
    cross_q, self_q, new_kv = [
        jnp.take(piece.reshape(wide_count * capacity, piece.shape[2]), target, axis=0)
        for piece in returned
    ]
    rows_total = steps * cand
    own_q = cross_q.reshape(rows_total, heads_dev, HEAD)
    scores = jnp.einsum("rhd,kd->rhk", own_q, keys, preferred_element_type=jnp.float32) * factor
    peak = jnp.max(scores, axis=-1, keepdims=True)
    expo = jnp.exp(scores - peak)
    total = jnp.sum(expo, axis=-1)
    result = (
        jnp.einsum(
            "rhk,kd->rhd", expo.astype(jnp.bfloat16), values, preferred_element_type=jnp.float32
        )
        / total[..., None]
    )
    cross_out = result.astype(jnp.bfloat16).reshape(1, steps, cand, heads_dev * HEAD)
    own_cand = cand // narrow_count
    queries = lax.all_to_all(
        self_q.reshape(steps, cand, self_q.shape[1]),
        "narrow",
        split_axis=1,
        concat_axis=2,
        tiled=True,
    )
    queries = queries.reshape(steps, own_cand, HEADS, HEAD)
    fresh = lax.dynamic_slice_in_dim(
        new_kv.reshape(steps, cand, new_kv.shape[1]), narrow_index * own_cand, own_cand, 1
    )
    cache = self_cache[0]
    prefix_scores = (
        jnp.einsum("tchd,cpd->tchp", queries, cache[..., :HEAD], preferred_element_type=jnp.float32)
        * factor
    )
    fresh_scores = (
        jnp.einsum("tchd,jcd->tchj", queries, fresh[..., :HEAD], preferred_element_type=jnp.float32)
        * factor
    )
    step_index = jnp.arange(steps, dtype=jnp.int32)
    allowed = (step_index[None, :] <= step_index[:, None])[:, None, None, :]
    fresh_masked = jnp.where(allowed, fresh_scores, -jnp.inf)
    peak = jnp.maximum(jnp.max(prefix_scores, axis=-1), jnp.max(fresh_masked, axis=-1))[..., None]
    prefix_expo = jnp.exp(prefix_scores - peak)
    fresh_expo = jnp.where(allowed, jnp.exp(fresh_masked - peak), 0.0)
    total = jnp.sum(prefix_expo, axis=-1) + jnp.sum(fresh_expo, axis=-1)
    summed = jnp.einsum(
        "tchp,cpd->tchd",
        prefix_expo.astype(jnp.bfloat16),
        cache[..., HEAD:],
        preferred_element_type=jnp.float32,
    )
    summed = summed + jnp.einsum(
        "tchj,jcd->tchd",
        fresh_expo.astype(jnp.bfloat16),
        fresh[..., HEAD:],
        preferred_element_type=jnp.float32,
    )
    self_result = summed / total[..., None]
    self_out = self_result.astype(jnp.bfloat16).reshape(1, steps, own_cand, HEADS * HEAD)
    return (cross_out, self_out)


def solution(mesh):
    placed = (
        P("wide", "narrow"),
        P("narrow"),
        P("narrow", None),
        P("wide"),
        P("wide", None, None),
        P("wide", "narrow"),
        P("wide", "narrow"),
        P("wide", None),
        P("wide", "narrow", None, None),
    )
    return jax.shard_map(
        body,
        mesh=mesh,
        in_specs=placed,
        out_specs=(P("wide", None, None, "narrow"), P("wide", None, "narrow", None)),
        check_vma=False,
    )
```

profile of v0, /device:TPU:24, one launch (start us, length us, event | category | flops | bytes accessed | tf_op | source)
XLA Modules:
  0.0 142.2 jit_solution(7858502208447242143)
XLA Ops:
  2.9 16.3 %all-to-all-start = ((s32[64,1,4]{2,1,0:T(1,128)}), s32[64,1,4]{2,1,0:T(1,128)S(1)}, u32[]{:S(2)}, u32[]{:S(2)}) async-start(s32[64,1,4]{2,1,0:T(1,128)} %bitcast), calls=%async_computation | async-start | bytes 65536 | tf_op jit(solution)/shard_map/all_to_all | solution.py:116
  19.3 1.1 fusion.27
  20.6 1.2 fusion.29
  22.6 6.0 %all-to-all-done = s32[64,1,4]{2,1,0:T(1,128)S(1)} async-done(((s32[64,1,4]{2,1,0:T(1,128)}), s32[64,1,4]{2,1,0:T(1,128)S(1)}, u32[]{:S(2)}, u32[]{:S(2)}) %all-to-all-start) | async-done | bytes 1056 | tf_op jit(solution)/shard_map/all_to_all | solution.py:116
  28.5 5.2 %all-to-all-start.2 = ((f32[8,24,257]{2,1,0:T(8,128)}), f32[8,24,257]{2,1,0:T(8,128)S(1)}, u32[]{:S(2)}, u32[]{:S(2)}) async-start(f32[8,24,257]{2,1,0:T(8,128)} %pad_maximum_fusion.1), calls=%async_computation.2 | async-start | bytes 589824 | tf_op jit(solution)/shard_map/all_to_all | solution.py:24
  35.3 1.2 gather_fusion
  36.5 1.2 gather_fusion.3
  37.7 1.2 gather_fusion.2
  39.5 1.3 pad_maximum_fusion
  41.4 7.2 %all-to-all-start.1 = ((bf16[64,4,1792]{2,1,0:T(4,128)(2,1)}), bf16[64,4,1792]{2,1,0:T(4,128)(2,1)S(1)}, u32[]{:S(2)}, u32[]{:S(2)}) async-start(bf16[64,4,1792]{2,1,0:T(4,128)(2,1)} %pad_maximum_fusion), calls=%async_computation.1 | async-start | bytes 1835008 | tf_op jit(solution)/shard_map/all_to_all | solution.py:60
  49.5 24.8 %all-to-all-done.1 = bf16[64,4,1792]{2,1,0:T(4,128)(2,1)S(1)} async-done(((bf16[64,4,1792]{2,1,0:T(4,128)(2,1)}), bf16[64,4,1792]{2,1,0:T(4,128)(2,1)S(1)}, u32[]{:S(2)}, u32[]{:S(2)}) %all-to-all-start.1) | async-done | bytes 917536 | tf_op jit(solution)/shard_map/all_to_all | solution.py:60
  74.4 0.9 broadcast_in_dim.142
  75.3 9.5 %all-to-all-start.3 = ((bf16[64,24,256]{2,1,0:T(8,128)(2,1)}), bf16[64,24,256]{2,1,0:T(8,128)(2,1)S(1)}, u32[]{:S(2)}, u32[]{:S(2)}) async-start(bf16[64,24,256]{2,1,0:T(8,128)(2,1)} %broadcast_in_dim.142), calls=%async_computation.3 | async-start | bytes 1572864 | tf_op jit(solution)/shard_map/all_to_all | solution.py:41
  89.4 18.6 %all-to-all-done.3 = bf16[64,24,256]{2,1,0:T(8,128)(2,1)S(1)} async-done(((bf16[64,24,256]{2,1,0:T(8,128)(2,1)}), bf16[64,24,256]{2,1,0:T(8,128)(2,1)S(1)}, u32[]{:S(2)}, u32[]{:S(2)}) %all-to-all-start.3) | async-done | bytes 786464 | tf_op jit(solution)/shard_map/all_to_all | solution.py:41
  108.0 4.8 %all-to-all-start.5 = ((bf16[2,64,768]{2,0,1:T(2,128)(2,1)}), bf16[2,64,768]{2,0,1:T(2,128)(2,1)S(1)}, u32[]{:S(2)}, u32[]{:S(2)}) async-start(bf16[2,64,768]{2,0,1:T(2,128)(2,1)} %copy.54), calls=%async_computation.5 | async-start | bytes 393216 | tf_op jit(solution)/shard_map/all_to_all | solution.py:148
  113.0 7.4 %all-to-all-done.5 = bf16[2,64,768]{2,0,1:T(2,128)(2,1)S(1)} async-done(((bf16[2,64,768]{2,0,1:T(2,128)(2,1)}), bf16[2,64,768]{2,0,1:T(2,128)(2,1)S(1)}, u32[]{:S(2)}, u32[]{:S(2)}) %all-to-all-start.5) | async-done | bytes 196640 | tf_op jit(solution)/shard_map/all_to_all | solution.py:148
  120.4 0.9 broadcast_in_dim.144
  121.3 3.7 %all-to-all-start.4 = ((bf16[8,8,24,256]{3,2,1,0:T(8,128)(2,1)}), bf16[8,8,24,256]{3,2,1,0:T(8,128)(2,1)S(1)}, u32[]{:S(2)}, u32[]{:S(2)}) async-start(bf16[8,8,24,256]{3,2,1,0:T(8,128)(2,1)} %broadcast_in_dim.144), calls=%async_computation.4 | async-start | bytes 1572864 | tf_op jit(solution)/shard_map/all_to_all | solution.py:41
  125.6 2.3 %bitcast_reduce_fusion = (f32[2,8,48]{2,0,1:T(2,128)S(1)}, f32[8,2,48,768]{3,2,1,0:T(8,128)S(1)}) fusion(bf16[2,8,48,128]{3,2,0,1:T(8,128)(2,1)S(1)} %reshape.320, bf16[8,768,256]{2,1,0:T(8,128)(2,1)} %bitcast.117), kind=kOutput, calls=%fused_computation.12 | convolution fusion | flops 152173824 | bytes 4131840 | tf_op jit(solution)/shard_map/tchd,cpd->tchp/dot_general | solution.py:161
  130.5 7.8 %all-to-all-done.4 = bf16[8,8,24,256]{3,2,1,0:T(8,128)(2,1)S(1)} async-done(((bf16[8,8,24,256]{3,2,1,0:T(8,128)(2,1)}), bf16[8,8,24,256]{3,2,1,0:T(8,128)(2,1)S(1)}, u32[]{:S(2)}, u32[]{:S(2)}) %all-to-all-start.4) | async-done | bytes 786464 | tf_op jit(solution)/shard_map/all_to_all | solution.py:41
  138.4 0.9 multiply_reduce_fusion
  139.3 0.9 fusion
  140.2 0.9 fusion.23
  141.3 0.9 reshape.317
  (81 shorter events, 14.1 us)
Async XLA Ops:
  0.6 20.0 %copy-start = (bf16[768,256]{1,0:T(8,128)(2,1)S(1)}, bf16[768,256]{1,0:T(8,128)(2,1)}, u32[]{:S(2)}) copy-start(bf16[768,256]{1,0:T(8,128)(2,1)} %param.15) | copy-start | bytes 1179652
  0.6 34.6 %copy-start.3 = (bf16[125,256]{1,0:T(8,128)(2,1)S(1)}, bf16[125,256]{1,0:T(8,128)(2,1)}, u32[]{:S(2)}) copy-start(bf16[125,256]{1,0:T(8,128)(2,1)} %param.20) | copy-start | bytes 192004
  0.7 35.8 %copy-start.1 = (bf16[125,768]{1,0:T(8,128)(2,1)S(1)}, bf16[125,768]{1,0:T(8,128)(2,1)}, u32[]{:S(2)}) copy-start(bf16[125,768]{1,0:T(8,128)(2,1)} %param.19) | copy-start | bytes 576004
  2.9 25.6 %all-to-all-start = ((s32[64,1,4]{2,1,0:T(1,128)}), s32[64,1,4]{2,1,0:T(1,128)S(1)}, u32[]{:S(2)}, u32[]{:S(2)}) async-start(s32[64,1,4]{2,1,0:T(1,128)} %bitcast), calls=%async_computation | async-start | bytes 65536 | tf_op jit(solution)/shard_map/all_to_all | solution.py:116
  28.5 12.8 %all-to-all-start.2 = ((f32[8,24,257]{2,1,0:T(8,128)}), f32[8,24,257]{2,1,0:T(8,128)S(1)}, u32[]{:S(2)}, u32[]{:S(2)}) async-start(f32[8,24,257]{2,1,0:T(8,128)} %pad_maximum_fusion.1), calls=%async_computation.2 | async-start | bytes 589824 | tf_op jit(solution)/shard_map/all_to_all | solution.py:24
  35.3 2.4 %copy-start.2 = (bf16[125,768]{1,0:T(8,128)(2,1)S(1)}, bf16[125,768]{1,0:T(8,128)(2,1)}, u32[]{:S(2)}) copy-start(bf16[125,768]{1,0:T(8,128)(2,1)} %param.18) | copy-start | bytes 576004
  40.8 44.0 %copy-start.5 = (s32[1,2,64]{2,1,0:T(2,128)S(1)}, s32[1,2,64]{2,1,0:T(2,128)}, u32[]{:S(2)}) copy-start(s32[1,2,64]{2,1,0:T(2,128)} %param.17) | copy-start | bytes 1540
  41.4 33.0 %all-to-all-start.1 = ((bf16[64,4,1792]{2,1,0:T(4,128)(2,1)}), bf16[64,4,1792]{2,1,0:T(4,128)(2,1)S(1)}, u32[]{:S(2)}, u32[]{:S(2)}) async-start(bf16[64,4,1792]{2,1,0:T(4,128)(2,1)} %pad_maximum_fusion), calls=%async_computation.1 | async-start | bytes 1835008 | tf_op jit(solution)/shard_map/all_to_all | solution.py:60
  75.3 32.7 %all-to-all-start.3 = ((bf16[64,24,256]{2,1,0:T(8,128)(2,1)}), bf16[64,24,256]{2,1,0:T(8,128)(2,1)S(1)}, u32[]{:S(2)}, u32[]{:S(2)}) async-start(bf16[64,24,256]{2,1,0:T(8,128)(2,1)} %broadcast_in_dim.142), calls=%async_computation.3 | async-start | bytes 1572864 | tf_op jit(solution)/shard_map/all_to_all | solution.py:41
  108.0 12.4 %all-to-all-start.5 = ((bf16[2,64,768]{2,0,1:T(2,128)(2,1)}), bf16[2,64,768]{2,0,1:T(2,128)(2,1)S(1)}, u32[]{:S(2)}, u32[]{:S(2)}) async-start(bf16[2,64,768]{2,0,1:T(2,128)(2,1)} %copy.54), calls=%async_computation.5 | async-start | bytes 393216 | tf_op jit(solution)/shard_map/all_to_all | solution.py:148
  121.3 17.0 %all-to-all-start.4 = ((bf16[8,8,24,256]{3,2,1,0:T(8,128)(2,1)}), bf16[8,8,24,256]{3,2,1,0:T(8,128)(2,1)S(1)}, u32[]{:S(2)}, u32[]{:S(2)}) async-start(bf16[8,8,24,256]{3,2,1,0:T(8,128)(2,1)} %broadcast_in_dim.144), calls=%async_computation.4 | async-start | bytes 1572864 | tf_op jit(solution)/shard_map/all_to_all | solution.py:41
  125.6 3.0 %copy-start.4 = (bf16[1,8,768,256]{3,2,1,0:T(8,128)(2,1)S(1)}, bf16[1,8,768,256]{3,2,1,0:T(8,128)(2,1)}, u32[]{:S(2)}) copy-start(bf16[1,8,768,256]{3,2,1,0:T(8,128)(2,1)} %param.21) | copy-start | bytes 9437188
where the time goes:
time: 143 us; the launch traced here: 142 us
  waiting for transfers between devices  65.2 us (46%)
  starting transfers between devices  46.7 us (33%)
  local copies, waits for them, and re-layouts  14.8 us (10%)
  other arithmetic  7.09 us (5%)
  matrix products  6.65 us (5%)
  between operations  1.74 us (1%)
    all_to_all x2, waiting for transfers between devices, copy_for_each(): lax.all_to_all(jnp.broadcast_to(shard[None], (length, *shard.shape)), axi...  26.4 us
    all_to_all x1, waiting for transfers between devices, in_one_piece(): lax.all_to_all(both, axis, split_axis=split_dim, concat_axis=concat_dim,...  24.8 us
    all_to_all x1, starting transfers between devices, body(): lax.all_to_all(request.reshape(wide_count, capacity), 'wide', split_axis=...  16.3 us
    all_to_all x2, starting transfers between devices, copy_for_each(): lax.all_to_all(jnp.broadcast_to(shard[None], (length, *shard.shape)), axi...  13.2 us
    all_to_all x1, waiting for transfers between devices, body(): lax.all_to_all(self_q.reshape(steps, cand, self_q.shape[1]), 'narrow', sp...  7.37 us
    all_to_all x1, starting transfers between devices, in_one_piece(): lax.all_to_all(both, axis, split_axis=split_dim, concat_axis=concat_dim,...  7.18 us
    all_to_all x1, waiting for transfers between devices, body(): lax.all_to_all(request.reshape(wide_count, capacity), 'wide', split_axis=...  5.97 us
    all_to_all x1, starting transfers between devices, sent_and_summed(): lax.all_to_all(pieces, axis, split_axis=0, concat_axis=0, tiled=True)  5.21 us
  transfers between devices with their start and end apart: 6, of which 6 were waited for; matrix products, arithmetic and copies ran while one was open for 14% of the time, Pallas kernels for 0%

commit v1 on v0

v1 whole, which is shorter than its diff:
```python
import jax
import jax.numpy as jnp
from jax import lax
from jax.experimental import pallas as pl
from jax.experimental.pallas import tpu as pltpu
from jax.sharding import Mesh
from jax.sharding import PartitionSpec as P

D = 6144
HEADS = 48
HEAD = 128
ENC_LEN = 1536
EPS = 1e-06
OWN = 125
PART = 8
CHUNK = 24
INTERPRET = False
F32 = jnp.float32
BF16 = jnp.bfloat16


def iota(shape, dim, dtype=F32):
    return lax.broadcasted_iota(jnp.int32, shape, dim).astype(dtype)


def call(kernel, outs, flops, **kw):
    return pl.pallas_call(
        kernel,
        out_shape=outs,
        interpret=INTERPRET,
        cost_estimate=pl.CostEstimate(flops=flops, bytes_accessed=1 << 20, transcendentals=0),
        **kw,
    )


def smem():
    return pl.BlockSpec(memory_space=pltpu.SMEM)


def vmem():
    return pl.BlockSpec(memory_space=pltpu.VMEM)


def onehot(hit):
    return jnp.where(hit, 1.0, 0.0).astype(BF16)


def pick(rows, table):
    return jnp.dot(rows, table, preferred_element_type=F32)


def request_kernel(assign_ref, ids_ref, req_ref, slot_ref):
    cand = ids_ref.shape[2]
    eye = iota((cand, cand), 0) == iota((cand, cand), 1)
    earlier = iota((cand, cand), 1) < iota((cand, cand), 0)
    lane = lax.broadcasted_iota(jnp.int32, (cand, 128), 1)
    lane_rank = jnp.where(lane < 8, lane & 3, 8).astype(F32)

    def column(row):
        return jnp.sum(jnp.where(eye, row, 0.0), axis=1, keepdims=True)

    total = jnp.zeros((64, 128), F32)
    own_rows = []
    for t in range(2):
        row = ids_ref[0, t : t + 1, :].astype(F32)
        own_row = jnp.floor((row + 0.5) * (1.0 / OWN))
        own = column(own_row)
        local = column(row) - own * OWN
        rank = jnp.sum(jnp.where(earlier & (own == own_row), 1.0, 0.0), axis=1, keepdims=True)
        for before in own_rows:
            rank = rank + jnp.sum(jnp.where(own == before, 1.0, 0.0), axis=1, keepdims=True)
        own_rows.append(own_row)
        slot_ref[t] = jnp.broadcast_to(own * 8.0 + rank, (cand, 128))
        left = onehot(iota((64, cand), 0) == own_row)
        right = jnp.where(rank == lane_rank, local + 1.0, 0.0)
        total = total + pick(left, right.astype(BF16))
    lane8 = lax.broadcasted_iota(jnp.int32, (64, 128), 1)
    asked = total - 1.0 + jnp.where((lane8 & 4) != 0, 128.0, 0.0)
    asked = jnp.where(total > 0.5, asked, -1.0)
    req_ref[...] = jnp.where(lane8 >= 64, assign_ref[0].astype(F32), asked)


def project_kernel(hidden_ref, gain_ref, weight_ref, out_ref):
    hidden = hidden_ref[...].astype(F32)
    scaled = (hidden * gain_ref[...]).astype(BF16)
    proj = jnp.dot(scaled, weight_ref[...], preferred_element_type=F32)
    squares = jnp.sum(hidden * hidden, axis=1, keepdims=True)
    lane = lax.broadcasted_iota(jnp.int32, (8, 256), 1)
    for k in range(PART):
        at = k * CHUNK
        out_ref[k, 0:CHUNK, :] = proj[at : at + CHUNK]
        tile = jnp.zeros((8, 256), F32)
        for m in range(CHUNK // 8):
            tile = jnp.where(lane == m, squares[at + 8 * m : at + 8 * m + 8], tile)
        out_ref[k, CHUNK : CHUNK + 8, :] = tile


def finish_kernel(arrived_ref, req_ref, out_ref):
    proj = arrived_ref[0, 0:CHUNK, :]
    squares = arrived_ref[0, CHUNK : CHUNK + 8, 0:128]
    for n in range(1, PART):
        proj = proj + arrived_ref[n, 0:CHUNK, :]
        squares = squares + arrived_ref[n, CHUNK : CHUNK + 8, 0:128]
    lane = lax.broadcasted_iota(jnp.int32, (8, 128), 1)
    row = lax.broadcasted_iota(jnp.int32, (8, 128), 0)
    parts = []
    for m in range(CHUNK // 8):
        total = jnp.sum(jnp.where(lane == m, squares, 0.0), axis=1, keepdims=True)
        parts.append(proj[8 * m : 8 * m + 8] * lax.rsqrt(total / D + EPS))
    whole = jnp.concatenate(parts, axis=0)
    for i in range(PART):
        three = whole[3 * i : 3 * i + 3]
        base = jnp.concatenate(
            [three[:, 0:HEAD], three[:, HEAD : 2 * HEAD], jnp.zeros((2, HEAD), F32)], axis=0
        )
        for p in range(PART):
            w = p * PART + i
            out_ref[w] = jnp.where(row == 6, req_ref[w : w + 1, :], base).astype(BF16)


def pack_kernel(place_ref, arrived_ref, cross_ref, self_ref, kv_ref, out_ref, table_ref, new_ref):
    outer = place_ref[0]
    rank = place_ref[2] >> 1
    table_ref[112:128, :] = jnp.zeros((16, table_ref.shape[1]), BF16)
    table_ref[240:256, :] = jnp.zeros((16, table_ref.shape[1]), BF16)
    new_ref[112:128, :] = jnp.zeros((16, HEAD), BF16)
    table_ref[0:OWN, :] = cross_ref[...]
    table_ref[128 : 128 + OWN, :] = self_ref[...]

    @pl.when((place_ref[2] & 1) == 0)
    def _():
        new_ref[0:OWN, :] = kv_ref[:, 0:HEAD]

    @pl.when((place_ref[2] & 1) == 1)
    def _():
        new_ref[0:OWN, :] = kv_ref[:, HEAD : 2 * HEAD]

    lane = lax.broadcasted_iota(jnp.int32, (64, 128), 1)
    j = lax.broadcasted_iota(jnp.int32, (64, 128), 0) & 7
    j_col = (lax.broadcasted_iota(jnp.int32, (64, 1), 0) & 7).astype(F32)
    want_extra = jnp.where(j == 6, rank, 64)
    outer_row = (outer * 8).astype(F32)
    lanes_table = iota((64, 256), 1)
    lanes_kv = iota((64, 512), 1)
    lanes_new = iota((64, 128), 1)
    for q in range(PART):
        at = 64 * q
        asked = arrived_ref[8 * q : 8 * q + 8].astype(F32)[:, 6:7, :]
        asked = jnp.broadcast_to(asked, (8, 8, 128)).reshape(64, 128)
        row = jnp.sum(jnp.where(lane == j, asked, 0.0), axis=1, keepdims=True)
        info = jnp.sum(jnp.where(lane == want_extra, asked, 0.0), axis=1, keepdims=True)
        own = jnp.where(j_col < 6.0, info * 64.0 + outer_row + j_col, -1.0)
        new = jnp.where(j_col == 6.0, info, -1.0)
        out_ref[at : at + 64, 0:768] = pick(onehot(lanes_table == row), table_ref[...]).astype(BF16)
        out_ref[at : at + 64, 768:896] = (
            pick(onehot(lanes_kv == own), arrived_ref[...].reshape(512, 128))
            + pick(onehot(lanes_new == new), new_ref[...])
        ).astype(BF16)


def unpack_kernel(place_ref, arrived_ref, slot_ref, cross_ref, out_ref):
    rank = (place_ref[2] >> 1).astype(F32)
    lanes = iota((128, 512), 1)
    spread = jnp.concatenate([slot_ref[0], slot_ref[1]], axis=0)[:, 0:1]
    cross_ref[...] = pick(onehot(lanes == spread), arrived_ref[:, 0:768]).astype(BF16)
    slot = jnp.concatenate(
        [slot_ref[t, 8 * k : 8 * k + 8] for k in range(PART) for t in range(2)], axis=0
    )[:, 0:1]
    self_q = pick(onehot(lanes == slot + 4.0), arrived_ref[:, 0:768]).astype(BF16)
    own_rank = slot - 8.0 * jnp.floor(slot * 0.125)
    piece = jnp.where(own_rank == rank, slot - own_rank + 6.0, -1.0)
    new = pick(onehot(lanes == piece), arrived_ref[:, 768:896]).astype(BF16)
    row = lax.broadcasted_iota(jnp.int32, (192, 512), 0)
    source = (row & 63) * 8 + (row >> 6)
    column = lax.broadcasted_iota(jnp.int32, (192, 512), 1)
    keys = pick(onehot(column == source), arrived_ref[:, 768:896]).astype(BF16)
    values = pick(onehot(column == source + 3), arrived_ref[:, 768:896]).astype(BF16)
    for k in range(PART):
        out_ref[k, :, 0:768] = self_q[16 * k : 16 * k + 16]
        out_ref[k, :, 768:896] = new[16 * k : 16 * k + 16]
        for m in range(12):
            at = 896 + 256 * m
            out_ref[k, :, at : at + 128] = keys[16 * m : 16 * m + 16]
            out_ref[k, :, at + 128 : at + 256] = values[16 * m : 16 * m + 16]


def exchange(
    enc_hidden, enc_gain, cross_weight, assign, token_ids, cross_table, self_table, kv_table
):
    place = jnp.stack([lax.axis_index("p"), lax.axis_index("i"), lax.axis_index("n")]).astype(
        jnp.int32
    )
    asked, slot = call(
        request_kernel,
        (jax.ShapeDtypeStruct((64, 128), F32), jax.ShapeDtypeStruct((2, 64, 128), F32)),
        1 << 20,
        in_specs=[smem(), vmem()],
        name="request",
    )(assign, token_ids)
    partial = call(
        project_kernel,
        jax.ShapeDtypeStruct((PART, CHUNK + 8, 256), F32),
        1 << 28,
        name="project",
    )(enc_hidden, enc_gain.reshape(1, -1), cross_weight)
    arrived = lax.all_to_all(partial, "n", 0, 0, tiled=True)
    finished = call(
        finish_kernel, jax.ShapeDtypeStruct((64, 8, 128), BF16), 1 << 20, name="finish"
    )(arrived, asked)
    arrived = lax.all_to_all(finished, ("p", "i"), 0, 0, tiled=True)
    packed = call(
        pack_kernel,
        jax.ShapeDtypeStruct((512, 896), BF16),
        1 << 28,
        in_specs=[smem(), vmem(), vmem(), vmem(), vmem()],
        scratch_shapes=[pltpu.VMEM((256, 768), BF16), pltpu.VMEM((128, 128), BF16)],
        name="pack",
    )(place, arrived, cross_table, self_table, kv_table)
    arrived = lax.all_to_all(packed.reshape(64, 8, 896), ("p", "i"), 0, 0, tiled=True)
    cross_q, message = call(
        unpack_kernel,
        (
            jax.ShapeDtypeStruct((128, 768), BF16),
            jax.ShapeDtypeStruct((PART, 16, 3968), BF16),
        ),
        1 << 28,
        in_specs=[smem(), vmem(), vmem()],
        name="unpack",
    )(place, arrived.reshape(512, 896), slot)
    arrived = lax.all_to_all(message, "n", 0, 0, tiled=True)
    return cross_q, arrived


def attend(cross_q, arrived, self_cache):
    factor = HEAD ** (-0.5)
    problem_kv = arrived[:, :, 896:].reshape(8, 16, 12, 256)
    problem_kv = jnp.transpose(problem_kv, (0, 2, 1, 3)).reshape(ENC_LEN, 256)
    keys = problem_kv[:, :HEAD]
    values = problem_kv[:, HEAD:]
    own_q = cross_q.reshape(128, 6, HEAD)
    scores = jnp.einsum("rhd,kd->rhk", own_q, keys, preferred_element_type=F32) * factor
    peak = jnp.max(scores, axis=-1, keepdims=True)
    expo = jnp.exp(scores - peak)
    total = jnp.sum(expo, axis=-1)
    result = (
        jnp.einsum("rhk,kd->rhd", expo.astype(BF16), values, preferred_element_type=F32)
        / total[..., None]
    )
    cross_out = result.astype(BF16).reshape(1, 2, 64, 768)

    queries = arrived[:, :, :768].reshape(8, 2, 8, 6, HEAD)
    queries = jnp.transpose(queries, (1, 2, 0, 3, 4)).reshape(2, 8, HEADS, HEAD)
    pieces = arrived[:, :, 768:896].astype(F32).reshape(4, 2, 2, 8, HEAD)
    fresh = jnp.sum(pieces, axis=0).astype(BF16)
    cache = self_cache[0]
    prefix_scores = (
        jnp.einsum("tchd,cpd->tchp", queries, cache[..., :HEAD], preferred_element_type=F32)
        * factor
    )
    fresh_scores = (
        jnp.einsum("tchd,jcd->tchj", queries, fresh[0], preferred_element_type=F32) * factor
    )
    step = jnp.arange(2, dtype=jnp.int32)
    allowed = (step[None, :] <= step[:, None])[:, None, None, :]
    fresh_masked = jnp.where(allowed, fresh_scores, -jnp.inf)
    peak = jnp.maximum(jnp.max(prefix_scores, axis=-1), jnp.max(fresh_masked, axis=-1))[..., None]
    prefix_expo = jnp.exp(prefix_scores - peak)
    fresh_expo = jnp.where(allowed, jnp.exp(fresh_masked - peak), 0.0)
    total = jnp.sum(prefix_expo, axis=-1) + jnp.sum(fresh_expo, axis=-1)
    summed = jnp.einsum(
        "tchp,cpd->tchd", prefix_expo.astype(BF16), cache[..., HEAD:], preferred_element_type=F32
    )
    summed = summed + jnp.einsum(
        "tchj,jcd->tchd", fresh_expo.astype(BF16), fresh[1], preferred_element_type=F32
    )
    self_out = (summed / total[..., None]).astype(BF16).reshape(1, 2, 8, HEADS * HEAD)
    return cross_out, self_out


def body(*args):
    cross_q, arrived = exchange(*args[:-1])
    return attend(cross_q, arrived, args[-1])


def specs():
    wide = ("p", "i")
    ins = (
        P(wide, "n"),
        P("n"),
        P("n", None),
        P(wide),
        P(wide, None, None),
        P(wide, "n"),
        P(wide, "n"),
        P(wide, None),
        P(wide, "n", None, None),
    )
    return ins, (P(wide, None, None, "n"), P(wide, None, "n", None))


def solution(mesh):
    cut = Mesh(mesh.devices.reshape(PART, PART, PART), ("p", "i", "n"))
    ins, outs = specs()
    return jax.shard_map(body, mesh=cut, in_specs=ins, out_specs=outs, check_vma=False)
```

time: 143 us -> 116 us (0.81)
  the two profiles are of different devices: /device:TPU:24 before, /device:TPU:1 now
where the time goes in v1:
time: 116 us
  blocking collectives  32.4 us (28%)
  waiting for transfers between devices  29.1 us (25%)
  starting transfers between devices  27.5 us (24%)
  Pallas kernels  11 us (9%)
  local copies, waits for them, and re-layouts  6.48 us (6%)
  matrix products  5.43 us (5%)
  other arithmetic  2.23 us (2%)
  between operations  1.44 us (1%)
    all_to_all x1, blocking collectives, exchange(): lax.all_to_all(packed.reshape(64, 8, 896), ('p', 'i'), 0, 0, tiled=True)  32.4 us
    all_to_all x1, starting transfers between devices, exchange(): arrived = lax.all_to_all(finished, ('p', 'i'), 0, 0, tiled=True)  17.3 us
    all_to_all x1, waiting for transfers between devices, exchange(): arrived = lax.all_to_all(message, 'n', 0, 0, tiled=True)  13 us
    all_to_all x1, waiting for transfers between devices, exchange(): arrived = lax.all_to_all(finished, ('p', 'i'), 0, 0, tiled=True)  12.1 us
    all_to_all x1, starting transfers between devices, exchange(): arrived = lax.all_to_all(partial, 'n', 0, 0, tiled=True)  6.65 us
    all_to_all x1, waiting for transfers between devices, exchange(): arrived = lax.all_to_all(partial, 'n', 0, 0, tiled=True)  3.89 us
    all_to_all x1, starting transfers between devices, exchange(): arrived = lax.all_to_all(message, 'n', 0, 0, tiled=True)  3.56 us
    pallas_call x1, Pallas kernels, exchange(): call(pack_kernel, jax.ShapeDtypeStruct((512, 896), BF16), 1 << 28, in_spe...  2.94 us
  transfers between devices with their start and end apart: 3, of which 3 were waited for; matrix products, arithmetic and copies ran while one was open for 1% of the time, Pallas kernels for 1%

profile of v1, /device:TPU:1, one launch (start us, length us, event | category | flops | bytes accessed | tf_op | source)
XLA Modules:
  0.0 115.6 jit_solution(1302296545808694508)
XLA Ops:
  0.6 1.3 %reshape.63.gain_ref = f32[1,768]{1,0:T(1,128)} reshape(f32[768]{0:T(1024)} %param.10) | data formatting | bytes 6144 | tf_op jit(solution)/shard_map/reshape | solution.py:205
  1.9 2.0 %project.1 = f32[8,32,256]{2,1,0:T(8,128)} custom-call(bf16[192,768]{1,0:T(8,128)(2,1)} %hidden_ref.1, f32[1,768]{1,0:T(1,128)} %reshape.63.gain_ref, bf16[768,256]{1,0:T(8,128)(2,1)} %weight_ref.1), custom_call_target="tpu_custom_call" | custom-call | flops 268435456 | bytes 1048576 | tf_op jit(solution)/shard_map/project/pallas_call | solution.py:200
  3.9 6.6 %all-to-all-start = ((f32[8,32,256]{2,1,0:T(8,128)}), f32[8,32,256]{2,1,0:T(8,128)S(1)}, u32[]{:S(2)}, u32[]{:S(2)}) async-start(f32[8,32,256]{2,1,0:T(8,128)} %project.1), calls=%async_computation | async-start | bytes 524288 | tf_op jit(solution)/shard_map/all_to_all | solution.py:206
  11.2 1.6 %request.1 = (f32[64,128]{1,0:T(8,128)}, f32[2,64,128]{2,1,0:T(8,128)}) custom-call(s32[1]{0:T(128)S(6)} %copy.54.assign_ref, s32[1,2,64]{2,1,0:T(2,128)} %ids_ref.1), custom_call_target="tpu_custom_call" | custom-call | flops 1048576 | bytes 1048576 | tf_op jit(solution)/shard_map/request/pallas_call | solution.py:193
  12.8 3.9 %all-to-all-done.arrived_ref = f32[8,32,256]{2,1,0:T(8,128)S(1)} async-done(((f32[8,32,256]{2,1,0:T(8,128)}), f32[8,32,256]{2,1,0:T(8,128)S(1)}, u32[]{:S(2)}, u32[]{:S(2)}) %all-to-all-start) | async-done | bytes 262176 | tf_op jit(solution)/shard_map/all_to_all | solution.py:206
  16.7 0.7 copy-done
  17.4 1.7 %finish.1 = bf16[64,8,128]{2,1,0:T(8,128)(2,1)} custom-call(f32[8,32,256]{2,1,0:T(8,128)} %copy-done, f32[64,128]{1,0:T(8,128)} %get-tuple-element.6.req_ref), custom_call_target="tpu_custom_call" | custom-call | flops 1048576 | bytes 1048576 | tf_op jit(solution)/shard_map/finish/pallas_call | solution.py:207
  19.1 17.3 %all-to-all-start.1 = ((bf16[64,8,128]{2,1,0:T(8,128)(2,1)}), bf16[64,8,128]{2,1,0:T(8,128)(2,1)S(1)}, u32[]{:S(2)}, u32[]{:S(2)}) async-start(bf16[64,8,128]{2,1,0:T(8,128)(2,1)} %finish.1), calls=%async_computation.1 | async-start | bytes 262144 | tf_op jit(solution)/shard_map/all_to_all | solution.py:210
  36.5 0.6 pad_add_fusion.place_ref
  37.1 12.1 %all-to-all-done.1.arrived_ref = bf16[64,8,128]{2,1,0:T(8,128)(2,1)S(1)} async-done(((bf16[64,8,128]{2,1,0:T(8,128)(2,1)}), bf16[64,8,128]{2,1,0:T(8,128)(2,1)S(1)}, u32[]{:S(2)}, u32[]{:S(2)}) %all-to-all-start.1) | async-done | bytes 131104 | tf_op jit(solution)/shard_map/all_to_all | solution.py:210
  49.2 0.7 copy-done.2
  49.9 2.9 %pack.1 = bf16[512,896]{1,0:T(8,128)(2,1)} custom-call(s32[3]{0:T(128)} %pad_add_fusion.place_ref, bf16[64,8,128]{2,1,0:T(8,128)(2,1)} %copy-done.2, bf16[125,768]{1,0:T(8,128)(2,1)} %cross_ref.1, bf16[125,768]{1,0:T(8,128)(2,1)} %self_ref.1, bf16[125,256]{1,0:T(8,128)(2,1)} %kv_ref.1), custom_call_target="tpu_custom_call" | custom-call | flops 268435456 | bytes 1048576 | tf_op jit(solution)/shard_map/pack/pallas_call | solution.py:211
  52.8 32.4 %all_to_all.20 = bf16[64,8,896]{2,1,0:T(8,128)(2,1)} all-to-all(bf16[64,8,896]{2,1,0:T(8,128)(2,1)} %bitcast.81), channel_id=1, replica_groups=mesh['p'=8,'i'=8,'n'=8] {'p','i'}, dimensions={0} | all-to-all | bytes 1835008 | tf_op jit(solution)/shard_map/all_to_all | solution.py:219
  85.2 2.7 %unpack.1 = (bf16[128,768]{1,0:T(8,128)(2,1)}, bf16[8,16,3968]{2,1,0:T(8,128)(2,1)}) custom-call(s32[3]{0:T(128)} %pad_add_fusion.place_ref, bf16[512,896]{1,0:T(8,128)(2,1)} %bitcast.84, f32[2,64,128]{2,1,0:T(8,128)} %get-tuple-element.7.slot_ref), custom_call_target="tpu_custom_call" | custom-call | flops 268435456 | bytes 1048576 | tf_op jit(solution)/shard_map/unpack/pallas_call | solution.py:220
  88.0 3.6 %all-to-all-start.3 = ((bf16[8,16,3968]{2,1,0:T(8,128)(2,1)}), bf16[8,16,3968]{2,1,0:T(8,128)(2,1)S(1)}, u32[]{:S(2)}, u32[]{:S(2)}) async-start(bf16[8,16,3968]{2,1,0:T(8,128)(2,1)} %get-tuple-element.9), calls=%async_computation.3 | async-start | bytes 2031616 | tf_op jit(solution)/shard_map/all_to_all | solution.py:230
  91.5 1.1 copy.23
  92.6 13.0 %all-to-all-done.3 = bf16[8,16,3968]{2,1,0:T(8,128)(2,1)S(1)} async-done(((bf16[8,16,3968]{2,1,0:T(8,128)(2,1)}), bf16[8,16,3968]{2,1,0:T(8,128)(2,1)S(1)}, u32[]{:S(2)}, u32[]{:S(2)}) %all-to-all-start.3) | async-done | bytes 1015840 | tf_op jit(solution)/shard_map/all_to_all | solution.py:230
  105.7 2.3 %bitcast_reduce_fusion = (f32[2,8,48]{2,0,1:T(2,128)S(1)}, f32[8,2,48,768]{3,2,1,0:T(8,128)S(1)}) fusion(bf16[8,768,256]{2,1,0:T(8,128)(2,1)} %bitcast.88, bf16[2,8,48,128]{3,1,2,0:T(8,128)(2,1)S(1)} %bitcast.86), kind=kOutput, calls=%fused_computation.6 | convolution fusion | flops 152173824 | bytes 4131840 | tf_op jit(solution)/shard_map/tchd,cpd->tchp/dot_general | solution.py:257
  109.0 0.7 fusion.13
  111.1 0.7 copy.32
  111.8 0.9 multiply_reduce_fusion
  112.7 0.9 fusion
  113.6 0.9 fusion.23
  114.7 0.9 reshape.69
  (21 shorter events, 2.5 us)
Async XLA Ops:
  3.9 12.8 %all-to-all-start = ((f32[8,32,256]{2,1,0:T(8,128)}), f32[8,32,256]{2,1,0:T(8,128)S(1)}, u32[]{:S(2)}, u32[]{:S(2)}) async-start(f32[8,32,256]{2,1,0:T(8,128)} %project.1), calls=%async_computation | async-start | bytes 524288 | tf_op jit(solution)/shard_map/all_to_all | solution.py:206
  16.7 0.7 copy-start
  19.1 30.1 %all-to-all-start.1 = ((bf16[64,8,128]{2,1,0:T(8,128)(2,1)}), bf16[64,8,128]{2,1,0:T(8,128)(2,1)S(1)}, u32[]{:S(2)}, u32[]{:S(2)}) async-start(bf16[64,8,128]{2,1,0:T(8,128)(2,1)} %finish.1), calls=%async_computation.1 | async-start | bytes 262144 | tf_op jit(solution)/shard_map/all_to_all | solution.py:210
  49.2 0.7 copy-start.2
  88.0 17.7 %all-to-all-start.3 = ((bf16[8,16,3968]{2,1,0:T(8,128)(2,1)}), bf16[8,16,3968]{2,1,0:T(8,128)(2,1)S(1)}, u32[]{:S(2)}, u32[]{:S(2)}) async-start(bf16[8,16,3968]{2,1,0:T(8,128)(2,1)} %get-tuple-element.9), calls=%async_computation.3 | async-start | bytes 2031616 | tf_op jit(solution)/shard_map/all_to_all | solution.py:230
  105.7 3.2 %copy-start.1 = (bf16[1,8,768,256]{3,2,1,0:T(8,128)(2,1)S(1)}, bf16[1,8,768,256]{3,2,1,0:T(8,128)(2,1)}, u32[]{:S(2)}) copy-start(bf16[1,8,768,256]{3,2,1,0:T(8,128)(2,1)} %param.17) | copy-start | bytes 9437188

commit v2 on v1

--- a/solution.py
+++ b/solution.py
@@ -9,11 +9,11 @@
 D = 6144
 HEADS = 48
 HEAD = 128
-ENC_LEN = 1536
 EPS = 1e-06
 OWN = 125
 PART = 8
 CHUNK = 24
+LOG2E = 1.4426950408889634
 INTERPRET = False
 F32 = jnp.float32
 BF16 = jnp.bfloat16
@@ -41,6 +41,14 @@
     return pl.BlockSpec(memory_space=pltpu.VMEM)
 
 
+def anywhere():
+    return pl.BlockSpec(memory_space=pl.ANY)
+
+
+def held(x):
+    return pltpu.with_memory_space_constraint(x, pltpu.VMEM)
+
+
 def onehot(hit):
     return jnp.where(hit, 1.0, 0.0).astype(BF16)
 
@@ -49,7 +57,7 @@
     return jnp.dot(rows, table, preferred_element_type=F32)
 
 
-def request_kernel(assign_ref, ids_ref, req_ref, slot_ref):
+def request(assign_ref, ids_ref, req_ref, slot_ref):
     cand = ids_ref.shape[2]
     eye = iota((cand, cand), 0) == iota((cand, cand), 1)
     earlier = iota((cand, cand), 1) < iota((cand, cand), 0)
@@ -80,9 +88,13 @@
     req_ref[...] = jnp.where(lane8 >= 64, assign_ref[0].astype(F32), asked)
 
 
-def project_kernel(hidden_ref, gain_ref, weight_ref, out_ref):
+def project_kernel(assign_ref, ids_ref, hidden_ref, gain_ref, weight_ref, *refs):
+    req_ref, slot_ref, out_ref = refs[3:6]
+    copies = [pltpu.make_async_copy(refs[k], refs[6 + k], refs[9].at[k]) for k in range(3)]
+    for copy in copies:
+        copy.start()
     hidden = hidden_ref[...].astype(F32)
-    scaled = (hidden * gain_ref[...]).astype(BF16)
+    scaled = (hidden * gain_ref[...].reshape(1, -1)).astype(BF16)
     proj = jnp.dot(scaled, weight_ref[...], preferred_element_type=F32)
     squares = jnp.sum(hidden * hidden, axis=1, keepdims=True)
     lane = lax.broadcasted_iota(jnp.int32, (8, 256), 1)
@@ -93,6 +105,9 @@
         for m in range(CHUNK // 8):
             tile = jnp.where(lane == m, squares[at + 8 * m : at + 8 * m + 8], tile)
         out_ref[k, CHUNK : CHUNK + 8, :] = tile
+    request(assign_ref, ids_ref, req_ref, slot_ref)
+    for copy in copies:
+        copy.wait()
 
 
 def finish_kernel(arrived_ref, req_ref, out_ref):
@@ -118,20 +133,21 @@
             out_ref[w] = jnp.where(row == 6, req_ref[w : w + 1, :], base).astype(BF16)
 
 
-def pack_kernel(place_ref, arrived_ref, cross_ref, self_ref, kv_ref, out_ref, table_ref, new_ref):
-    outer = place_ref[0]
-    rank = place_ref[2] >> 1
+def pack_kernel(arrived_ref, cross_ref, self_ref, kv_ref, out_ref, table_ref, new_ref):
+    outer = lax.axis_index("p")
+    narrow = lax.axis_index("n")
+    rank = narrow >> 1
     table_ref[112:128, :] = jnp.zeros((16, table_ref.shape[1]), BF16)
     table_ref[240:256, :] = jnp.zeros((16, table_ref.shape[1]), BF16)
     new_ref[112:128, :] = jnp.zeros((16, HEAD), BF16)
     table_ref[0:OWN, :] = cross_ref[...]
     table_ref[128 : 128 + OWN, :] = self_ref[...]
 
-    @pl.when((place_ref[2] & 1) == 0)
+    @pl.when((narrow & 1) == 0)
     def _():
         new_ref[0:OWN, :] = kv_ref[:, 0:HEAD]
 
-    @pl.when((place_ref[2] & 1) == 1)
+    @pl.when((narrow & 1) == 1)
     def _():
         new_ref[0:OWN, :] = kv_ref[:, HEAD : 2 * HEAD]
 
@@ -158,8 +174,8 @@
         ).astype(BF16)
 
 
-def unpack_kernel(place_ref, arrived_ref, slot_ref, cross_ref, out_ref):
-    rank = (place_ref[2] >> 1).astype(F32)
+def unpack_kernel(arrived_ref, slot_ref, cross_ref, out_ref):
+    rank = (lax.axis_index("n") >> 1).astype(F32)
     lanes = iota((128, 512), 1)
     spread = jnp.concatenate([slot_ref[0], slot_ref[1]], axis=0)[:, 0:1]
     cross_ref[...] = pick(onehot(lanes == spread), arrived_ref[:, 0:768]).astype(BF16)
@@ -187,94 +203,155 @@
 def exchange(
     enc_hidden, enc_gain, cross_weight, assign, token_ids, cross_table, self_table, kv_table
 ):
-    place = jnp.stack([lax.axis_index("p"), lax.axis_index("i"), lax.axis_index("n")]).astype(
-        jnp.int32
+    tables = (cross_table, self_table, kv_table)
+    asked, slot, partial, *tables = call(
+        project_kernel,
+        (
+            pltpu.VMEM((64, 128), F32),
+            pltpu.VMEM((2, 64, 128), F32),
+            pltpu.VMEM((PART, CHUNK + 8, 256), F32),
+            *[pltpu.VMEM(x.shape, x.dtype) for x in tables],
+        ),
+        1 << 28,
+        in_specs=[smem(), vmem(), vmem(), vmem(), vmem(), anywhere(), anywhere(), anywhere()],
+        scratch_shapes=[pltpu.SemaphoreType.DMA((3,))],
+        name="project",
+    )(assign, token_ids, enc_hidden, enc_gain, cross_weight, *tables)
+    arrived = lax.all_to_all(partial, "n", 0, 0, tiled=True)
+    finished = call(finish_kernel, pltpu.VMEM((64, 8, 128), BF16), 1 << 20, name="finish")(
+        held(arrived), held(asked)
     )
-    asked, slot = call(
-        request_kernel,
-        (jax.ShapeDtypeStruct((64, 128), F32), jax.ShapeDtypeStruct((2, 64, 128), F32)),
-        1 << 20,
-        in_specs=[smem(), vmem()],
-        name="request",
-    )(assign, token_ids)
-    partial = call(
-        project_kernel,
-        jax.ShapeDtypeStruct((PART, CHUNK + 8, 256), F32),
-        1 << 28,
-        name="project",
-    )(enc_hidden, enc_gain.reshape(1, -1), cross_weight)
-    arrived = lax.all_to_all(partial, "n", 0, 0, tiled=True)
-    finished = call(
-        finish_kernel, jax.ShapeDtypeStruct((64, 8, 128), BF16), 1 << 20, name="finish"
-    )(arrived, asked)
     arrived = lax.all_to_all(finished, ("p", "i"), 0, 0, tiled=True)
     packed = call(
         pack_kernel,
-        jax.ShapeDtypeStruct((512, 896), BF16),
+        pltpu.VMEM((512, 896), BF16),
         1 << 28,
-        in_specs=[smem(), vmem(), vmem(), vmem(), vmem()],
         scratch_shapes=[pltpu.VMEM((256, 768), BF16), pltpu.VMEM((128, 128), BF16)],
         name="pack",
-    )(place, arrived, cross_table, self_table, kv_table)
+    )(held(arrived), *[held(x) for x in tables])
     arrived = lax.all_to_all(packed.reshape(64, 8, 896), ("p", "i"), 0, 0, tiled=True)
     cross_q, message = call(
         unpack_kernel,
+        (pltpu.VMEM((128, 768), BF16), pltpu.VMEM((PART, 16, 3968), BF16)),
+        1 << 28,
+        name="unpack",
+    )(held(arrived.reshape(512, 896)), held(slot))
+    arrived = lax.all_to_all(message, "n", 0, 0, tiled=True)
+    return cross_q, arrived
+
+
+def attend_kernel(
+    query_ref,
+    arrived_ref,
+    far_cache_ref,
+    cross_ref,
+    self_ref,
+    stack_ref,
+    key_ref,
+    value_ref,
+    own_ref,
+    result_ref,
+    cache_ref,
+    arrival,
+):
+    fetch = pltpu.make_async_copy(far_cache_ref, cache_ref, arrival)
+    fetch.start()
+    scale = LOG2E * HEAD ** (-0.5)
+    across = (((1,), (1,)), ((), ()))
+
+    for n in range(PART):
+        for m in range(12):
+            at, lane = 192 * n + 16 * m, 896 + 256 * m
+            key_ref[at : at + 16, :] = arrived_ref[n, :, lane : lane + HEAD]
+            value_ref[at : at + 16, :] = arrived_ref[n, :, lane + HEAD : lane + 2 * HEAD]
+    for h in range(6):
+        stack_ref[128 * h : 128 * h + 128, :] = query_ref[:, h * HEAD : (h + 1) * HEAD]
+
+    for b in range(2):
+        query = stack_ref[384 * b : 384 * b + 384, :]
+        scores = [
+            lax.dot_general(
+                query, key_ref[512 * k : 512 * k + 512, :], across, preferred_element_type=F32
+            )
+            for k in range(3)
+        ]
+        peak = jnp.max(scores[0], axis=1, keepdims=True)
+        for s in scores[1:]:
+            peak = jnp.maximum(peak, jnp.max(s, axis=1, keepdims=True))
+        total = jnp.zeros((384, 1), F32)
+        result = jnp.zeros((384, HEAD), F32)
+        for k in range(3):
+            expo = jnp.exp2((scores[k] - peak) * scale)
+            total = total + jnp.sum(expo, axis=1, keepdims=True)
+            result = result + pick(expo.astype(BF16), value_ref[512 * k : 512 * k + 512, :])
+        result = (result / total).astype(BF16)
+        for h in range(3):
+            at = (3 * b + h) * HEAD
+            cross_ref[:, at : at + HEAD] = result[128 * h : 128 * h + 128]
+
+    new_key = arrived_ref[0, :, 768:896].astype(F32)
+    new_value = arrived_ref[1, :, 768:896].astype(F32)
+    for n in range(2, PART, 2):
+        new_key = new_key + arrived_ref[n, :, 768:896].astype(F32)
+        new_value = new_value + arrived_ref[n + 1, :, 768:896].astype(F32)
+    for n in range(PART):
+        for h in range(6):
+            tile = arrived_ref[n, :, h * HEAD : (h + 1) * HEAD].astype(F32)
+            for t in range(2):
+                at = 8 * (48 * t + 6 * n + h)
+                own_ref[at : at + 8, :] = tile[8 * t : 8 * t + 8]
+
+    fetch.wait()
+    second = lax.broadcasted_iota(jnp.int32, (96, 1), 0) >= 48
+    for c in range(8):
+        query = own_ref[pl.ds(c, 96, stride=8), :]
+        scores = lax.dot_general(
+            query.astype(BF16), cache_ref[c, :, 0:HEAD], across, preferred_element_type=F32
+        )
+        fresh = [
+            jnp.sum(query * new_key[8 * j + c : 8 * j + c + 1], axis=1, keepdims=True)
+            for j in range(2)
+        ]
+        fresh[1] = jnp.where(second, fresh[1], -jnp.inf)
+        peak = jnp.max(scores, axis=1, keepdims=True)
+        peak = jnp.maximum(peak, jnp.maximum(fresh[0], fresh[1]))
+        expo = jnp.exp2((scores - peak) * scale)
+        total = jnp.sum(expo, axis=1, keepdims=True)
+        result = pick(expo.astype(BF16), cache_ref[c, :, HEAD : 2 * HEAD])
+        for j in range(2):
+            weight = jnp.exp2((fresh[j] - peak) * scale)
+            total = total + weight
+            rounded = weight.astype(BF16).astype(F32)
+            result = result + rounded * new_value[8 * j + c : 8 * j + c + 1]
+        result_ref[pl.ds(c, 96, stride=8), :] = result / total
+
+    for t in range(2):
+        for h in range(HEADS):
+            at = 8 * (HEADS * t + h)
+            self_ref[t, :, h * HEAD : (h + 1) * HEAD] = result_ref[at : at + 8, :].astype(BF16)
+
+
+def attend(cross_q, arrived, self_cache):
+    cross_out, self_out = call(
+        attend_kernel,
         (
             jax.ShapeDtypeStruct((128, 768), BF16),
-            jax.ShapeDtypeStruct((PART, 16, 3968), BF16),
+            jax.ShapeDtypeStruct((2, 8, HEADS * HEAD), BF16),
         ),
-        1 << 28,
-        in_specs=[smem(), vmem(), vmem()],
-        name="unpack",
-    )(place, arrived.reshape(512, 896), slot)
-    arrived = lax.all_to_all(message, "n", 0, 0, tiled=True)
-    return cross_q, arrived
-
-
-def attend(cross_q, arrived, self_cache):
-    factor = HEAD ** (-0.5)
-    problem_kv = arrived[:, :, 896:].reshape(8, 16, 12, 256)
-    problem_kv = jnp.transpose(problem_kv, (0, 2, 1, 3)).reshape(ENC_LEN, 256)
-    keys = problem_kv[:, :HEAD]
-    values = problem_kv[:, HEAD:]
-    own_q = cross_q.reshape(128, 6, HEAD)
-    scores = jnp.einsum("rhd,kd->rhk", own_q, keys, preferred_element_type=F32) * factor
-    peak = jnp.max(scores, axis=-1, keepdims=True)
-    expo = jnp.exp(scores - peak)
-    total = jnp.sum(expo, axis=-1)
-    result = (
-        jnp.einsum("rhk,kd->rhd", expo.astype(BF16), values, preferred_element_type=F32)
-        / total[..., None]
-    )
-    cross_out = result.astype(BF16).reshape(1, 2, 64, 768)
-
-    queries = arrived[:, :, :768].reshape(8, 2, 8, 6, HEAD)
-    queries = jnp.transpose(queries, (1, 2, 0, 3, 4)).reshape(2, 8, HEADS, HEAD)
-    pieces = arrived[:, :, 768:896].astype(F32).reshape(4, 2, 2, 8, HEAD)
-    fresh = jnp.sum(pieces, axis=0).astype(BF16)
-    cache = self_cache[0]
-    prefix_scores = (
-        jnp.einsum("tchd,cpd->tchp", queries, cache[..., :HEAD], preferred_element_type=F32)
-        * factor
-    )
-    fresh_scores = (
-        jnp.einsum("tchd,jcd->tchj", queries, fresh[0], preferred_element_type=F32) * factor
-    )
-    step = jnp.arange(2, dtype=jnp.int32)
-    allowed = (step[None, :] <= step[:, None])[:, None, None, :]
-    fresh_masked = jnp.where(allowed, fresh_scores, -jnp.inf)
-    peak = jnp.maximum(jnp.max(prefix_scores, axis=-1), jnp.max(fresh_masked, axis=-1))[..., None]
-    prefix_expo = jnp.exp(prefix_scores - peak)
-    fresh_expo = jnp.where(allowed, jnp.exp(fresh_masked - peak), 0.0)
-    total = jnp.sum(prefix_expo, axis=-1) + jnp.sum(fresh_expo, axis=-1)
-    summed = jnp.einsum(
-        "tchp,cpd->tchd", prefix_expo.astype(BF16), cache[..., HEAD:], preferred_element_type=F32
-    )
-    summed = summed + jnp.einsum(
-        "tchj,jcd->tchd", fresh_expo.astype(BF16), fresh[1], preferred_element_type=F32
-    )
-    self_out = (summed / total[..., None]).astype(BF16).reshape(1, 2, 8, HEADS * HEAD)
-    return cross_out, self_out
+        1 << 30,
+        scratch_shapes=[
+            pltpu.VMEM((768, HEAD), BF16),
+            pltpu.VMEM((1536, HEAD), BF16),
+            pltpu.VMEM((1536, HEAD), BF16),
+            pltpu.VMEM((768, HEAD), F32),
+            pltpu.VMEM((768, HEAD), F32),
+            pltpu.VMEM(self_cache.shape[1:], BF16),
+            pltpu.SemaphoreType.DMA,
+        ],
+        in_specs=[vmem(), vmem(), anywhere()],
+        name="attend",
+    )(held(cross_q), held(arrived), self_cache[0])
+    return cross_out.reshape(1, 2, 64, 768), self_out[None]
 
 
 def body(*args):

time: 116 us -> 102 us (0.88)
  blocking collectives: 32.4 us -> 90.6 us
  waiting for transfers between devices: 29.1 us -> 0 us
  starting transfers between devices: 27.5 us -> 0 us
  local copies, waits for them, and re-layouts: 6.48 us -> 0 us
  matrix products: 5.43 us -> 0 us
  other arithmetic: 2.23 us -> 0 us
  Pallas kernels: 11 us -> 9.36 us
    all_to_all x0 -> x3, blocking collectives: none -> 59.3 us  [the longest x1 29.9 us: exchange(): arrived = lax.all_to_all(finished, ('p', 'i'), 0, 0, tiled=True)]
    all_to_all x3 -> x0, waiting for transfers between devices: 29.1 us -> none  [the longest x1 13 us: exchange(): arrived = lax.all_to_all(message, 'n', 0, 0, tiled=True)]
    all_to_all x3 -> x0, starting transfers between devices: 27.5 us -> none  [the longest x1 17.3 us: exchange(): arrived = lax.all_to_all(finished, ('p', 'i'), 0, 0, tiled=True)]
    dot_general x6 -> x0, matrix products: 5.43 us -> none  [the longest x1 2.27 us: attend(): jnp.einsum('tchd,cpd->tchp', queries, cache[..., :HEAD], preferred_elemen...]
    reshape x6 -> x0, local copies, waits for them, and re-layouts: 2.79 us -> none  [the longest x1 1.27 us: exchange(): enc_gain.reshape(1, -1)]
    unnamed x7 -> x0, local copies, waits for them, and re-layouts: 2.09 us -> none
    pallas_call x5, Pallas kernels: 11 us -> 9.36 us  [the longest x1 5.6 us: attend(): call(attend_kernel, (jax.ShapeDtypeStruct((128, 768), BF16), jax.ShapeDty...]
    reduce_sum x4 -> x0, other arithmetic: 1.61 us -> none  [the longest x1 0.91 us: attend(): total = jnp.sum(expo, axis=-1)]
  transfers between devices with their start and end apart: 3 -> 0, of which waited for: 3 -> 0; matrix products, arithmetic and copies ran while one was open for 1% -> 0% of each run, Pallas kernels for 1% -> 0%
where the time goes in v2:
time: 102 us; the launch traced here: 101 us
  blocking collectives  90.6 us (89%)
  Pallas kernels  9.36 us (9%)
  between operations  1.31 us (1%)
    all_to_all x1, blocking collectives, exchange(): lax.all_to_all(packed.reshape(64, 8, 896), ('p', 'i'), 0, 0, tiled=True)  31.3 us
    all_to_all x1, blocking collectives, exchange(): arrived = lax.all_to_all(finished, ('p', 'i'), 0, 0, tiled=True)  29.9 us
    all_to_all x1, blocking collectives, exchange(): arrived = lax.all_to_all(message, 'n', 0, 0, tiled=True)  16.9 us
    all_to_all x1, blocking collectives, exchange(): arrived = lax.all_to_all(partial, 'n', 0, 0, tiled=True)  12.6 us
    pallas_call x1, Pallas kernels, attend(): call(attend_kernel, (jax.ShapeDtypeStruct((128, 768), BF16), jax.ShapeDty...  5.6 us
    pallas_call x1, Pallas kernels, exchange(): call(project_kernel, (pltpu.VMEM((64, 128), F32), pltpu.VMEM((2, 64, 128)...  2.19 us

profile of v2, /device:TPU:1, one launch (start us, length us, event | category | flops | bytes accessed | tf_op | source)
XLA Modules:
  0.0 101.2 jit_solution(5036399882189636352)
XLA Ops:
  1.3 2.2 %project.1 = (f32[64,128]{1,0:T(8,128)S(1)}, f32[2,64,128]{2,1,0:T(8,128)S(1)}, f32[8,32,256]{2,1,0:T(8,128)S(1)}, bf16[125,768]{1,0:T(8,128)(2,1)S(1)}, bf16[12...) custom-call(s32[1]{0:T(128)S(6)} %copy.11.assign_ref, s32[1,2,64]{2,1,0:T(2,128)} %ids_ref.1, ...), custom_call_target="tpu_custom_call" | custom-call | flops 268435456 | bytes 1048576 | tf_op jit(solution)/shard_map/project/pallas_call | solution.py:207
  3.5 12.6 %all_to_all.20.arrived_ref = f32[8,32,256]{2,1,0:T(8,128)S(1)} all-to-all(f32[8,32,256]{2,1,0:T(8,128)S(1)} %get-tuple-element.12), channel_id=1, replica_groups=mesh['p'=8,'i'=8,'n'=8] {'n'}, dimensions={0} | all-to-all | bytes 524288 | tf_op jit(solution)/shard_map/all_to_all | solution.py:220
  16.1 0.1 finish.1
  16.2 29.9 %all_to_all.21.arrived_ref = bf16[64,8,128]{2,1,0:T(8,128)(2,1)S(1)} all-to-all(bf16[64,8,128]{2,1,0:T(8,128)(2,1)S(1)} %finish.1), channel_id=1, replica_groups=mesh['p'=8,'i'=8,'n'=8] {'p','i'}, dimensions={0} | all-to-all | bytes 262144 | tf_op jit(solution)/shard_map/all_to_all | solution.py:224
  46.0 0.9 pack.1
  46.9 31.3 %all_to_all.22 = bf16[64,8,896]{2,1,0:T(8,128)(2,1)S(1)} all-to-all(bf16[64,8,896]{2,1,0:T(8,128)(2,1)S(1)} %bitcast.5), channel_id=1, replica_groups=mesh['p'=8,'i'=8,'n'=8] {'p','i'}, dimensions={0} | all-to-all | bytes 1835008 | tf_op jit(solution)/shard_map/all_to_all | solution.py:232
  78.2 0.6 unpack.1
  78.8 16.9 %all_to_all.23.arrived_ref = bf16[8,16,3968]{2,1,0:T(8,128)(2,1)S(1)} all-to-all(bf16[8,16,3968]{2,1,0:T(8,128)(2,1)S(1)} %get-tuple-element.19), channel_id=1, replica_groups=mesh['p'=8,'i'=8,'n'=8] {'n'}, dimensions={0} | all-to-all | bytes 2031616 | tf_op jit(solution)/shard_map/all_to_all | solution.py:239
  95.6 5.6 %attend.1 = (bf16[128,768]{1,0:T(8,128)(2,1)}, bf16[2,8,6144]{2,1,0:T(8,128)(2,1)}) custom-call(bf16[128,768]{1,0:T(8,128)(2,1)S(1)} %get-tuple-element.18.query_ref, bf16[8,16,3968]{2,1,0:T(8,128)(2,1)S(1)} %all_to_all.23.arrived_ref, bf16[8,768,256]{2,1,0:T(8,128)(2,1)} %bitcast.7), custom_call_target="tpu_custom_call" | custom-call | flops 1073741824 | bytes 1048576 | tf_op jit(solution)/shard_map/attend/pallas_call | solution.py:335

commit v3 on v2

--- a/solution.py
+++ b/solution.py
@@ -85,43 +85,47 @@
     lane8 = lax.broadcasted_iota(jnp.int32, (64, 128), 1)
     asked = total - 1.0 + jnp.where((lane8 & 4) != 0, 128.0, 0.0)
     asked = jnp.where(total > 0.5, asked, -1.0)
-    req_ref[...] = jnp.where(lane8 >= 64, assign_ref[0].astype(F32), asked)
-
-
-def project_kernel(assign_ref, ids_ref, hidden_ref, gain_ref, weight_ref, *refs):
+    problem = assign_ref[...].astype(F32).reshape(1, 1)
+    req_ref[...] = jnp.where(lane8 >= 64, problem, asked)
+
+
+def project_kernel(assign_ref, ids_ref, gain_ref, far_hidden_ref, far_weight_ref, *refs):
     req_ref, slot_ref, out_ref = refs[3:6]
-    copies = [pltpu.make_async_copy(refs[k], refs[6 + k], refs[9].at[k]) for k in range(3)]
+    far = (far_hidden_ref, far_weight_ref, *refs[0:3])
+    hidden_ref, weight_ref = refs[9:11]
+    near = (hidden_ref, weight_ref, *refs[6:9])
+    copies = [pltpu.make_async_copy(far[k], near[k], refs[11].at[k]) for k in range(5)]
     for copy in copies:
         copy.start()
+    copies[0].wait()
     hidden = hidden_ref[...].astype(F32)
     scaled = (hidden * gain_ref[...].reshape(1, -1)).astype(BF16)
+    copies[1].wait()
     proj = jnp.dot(scaled, weight_ref[...], preferred_element_type=F32)
     squares = jnp.sum(hidden * hidden, axis=1, keepdims=True)
-    lane = lax.broadcasted_iota(jnp.int32, (8, 256), 1)
+    lane = lax.broadcasted_iota(jnp.int32, (8, 128), 1)
     for k in range(PART):
-        at = k * CHUNK
-        out_ref[k, 0:CHUNK, :] = proj[at : at + CHUNK]
-        tile = jnp.zeros((8, 256), F32)
+        tile = jnp.zeros((8, 128), F32)
         for m in range(CHUNK // 8):
-            tile = jnp.where(lane == m, squares[at + 8 * m : at + 8 * m + 8], tile)
-        out_ref[k, CHUNK : CHUNK + 8, :] = tile
+            at = k * CHUNK + 8 * m
+            out_ref[k, :, 256 * m : 256 * m + 256] = proj[at : at + 8]
+            tile = jnp.where(lane == m, squares[at : at + 8], tile)
+        out_ref[k, :, 768:896] = tile
     request(assign_ref, ids_ref, req_ref, slot_ref)
-    for copy in copies:
+    for copy in copies[2:]:
         copy.wait()
 
 
 def finish_kernel(arrived_ref, req_ref, out_ref):
-    proj = arrived_ref[0, 0:CHUNK, :]
-    squares = arrived_ref[0, CHUNK : CHUNK + 8, 0:128]
+    message = arrived_ref[0]
     for n in range(1, PART):
-        proj = proj + arrived_ref[n, 0:CHUNK, :]
-        squares = squares + arrived_ref[n, CHUNK : CHUNK + 8, 0:128]
+        message = message + arrived_ref[n]
     lane = lax.broadcasted_iota(jnp.int32, (8, 128), 1)
     row = lax.broadcasted_iota(jnp.int32, (8, 128), 0)
     parts = []
     for m in range(CHUNK // 8):
-        total = jnp.sum(jnp.where(lane == m, squares, 0.0), axis=1, keepdims=True)
-        parts.append(proj[8 * m : 8 * m + 8] * lax.rsqrt(total / D + EPS))
+        total = jnp.sum(jnp.where(lane == m, message[:, 768:896], 0.0), axis=1, keepdims=True)
+        parts.append(message[:, 256 * m : 256 * m + 256] * lax.rsqrt(total / D + EPS))
     whole = jnp.concatenate(parts, axis=0)
     for i in range(PART):
         three = whole[3 * i : 3 * i + 3]
@@ -209,14 +213,18 @@
         (
             pltpu.VMEM((64, 128), F32),
             pltpu.VMEM((2, 64, 128), F32),
-            pltpu.VMEM((PART, CHUNK + 8, 256), F32),
+            pltpu.VMEM((PART, 8, 896), F32),
             *[pltpu.VMEM(x.shape, x.dtype) for x in tables],
         ),
         1 << 28,
-        in_specs=[smem(), vmem(), vmem(), vmem(), vmem(), anywhere(), anywhere(), anywhere()],
-        scratch_shapes=[pltpu.SemaphoreType.DMA((3,))],
+        in_specs=[vmem(), vmem(), vmem(), *[anywhere()] * 5],
+        scratch_shapes=[
+            pltpu.VMEM(enc_hidden.shape, BF16),
+            pltpu.VMEM(cross_weight.shape, BF16),
+            pltpu.SemaphoreType.DMA((5,)),
+        ],
         name="project",
-    )(assign, token_ids, enc_hidden, enc_gain, cross_weight, *tables)
+    )(assign, token_ids, enc_gain, enc_hidden, cross_weight, *tables)
     arrived = lax.all_to_all(partial, "n", 0, 0, tiled=True)
     finished = call(finish_kernel, pltpu.VMEM((64, 8, 128), BF16), 1 << 20, name="finish")(
         held(arrived), held(asked)
@@ -264,29 +272,35 @@
             at, lane = 192 * n + 16 * m, 896 + 256 * m
             key_ref[at : at + 16, :] = arrived_ref[n, :, lane : lane + HEAD]
             value_ref[at : at + 16, :] = arrived_ref[n, :, lane + HEAD : lane + 2 * HEAD]
+
     for h in range(6):
         stack_ref[128 * h : 128 * h + 128, :] = query_ref[:, h * HEAD : (h + 1) * HEAD]
-
-    for b in range(2):
-        query = stack_ref[384 * b : 384 * b + 384, :]
-        scores = [
+    def begin(b):
+        query = stack_ref[256 * b : 256 * b + 256, :]
+        return [
             lax.dot_general(
                 query, key_ref[512 * k : 512 * k + 512, :], across, preferred_element_type=F32
             )
             for k in range(3)
         ]
+
+    scores_ahead = begin(0)
+    for b in range(3):
+        scores = scores_ahead
+        if b < 2:
+            scores_ahead = begin(b + 1)
         peak = jnp.max(scores[0], axis=1, keepdims=True)
         for s in scores[1:]:
             peak = jnp.maximum(peak, jnp.max(s, axis=1, keepdims=True))
-        total = jnp.zeros((384, 1), F32)
-        result = jnp.zeros((384, HEAD), F32)
+        total = jnp.zeros((256, 1), F32)
+        result = jnp.zeros((256, HEAD), F32)
         for k in range(3):
             expo = jnp.exp2((scores[k] - peak) * scale)
             total = total + jnp.sum(expo, axis=1, keepdims=True)
             result = result + pick(expo.astype(BF16), value_ref[512 * k : 512 * k + 512, :])
         result = (result / total).astype(BF16)
-        for h in range(3):
-            at = (3 * b + h) * HEAD
+        for h in range(2):
+            at = (2 * b + h) * HEAD
             cross_ref[:, at : at + HEAD] = result[128 * h : 128 * h + 128]
 
     new_key = arrived_ref[0, :, 768:896].astype(F32)
@@ -303,11 +317,19 @@
 
     fetch.wait()
     second = lax.broadcasted_iota(jnp.int32, (96, 1), 0) >= 48
-    for c in range(8):
+
+    def start(c):
         query = own_ref[pl.ds(c, 96, stride=8), :]
         scores = lax.dot_general(
             query.astype(BF16), cache_ref[c, :, 0:HEAD], across, preferred_element_type=F32
         )
+        return query, scores
+
+    ahead = [start(0), start(1)]
+    for c in range(8):
+        query, scores = ahead.pop(0)
+        if c < 6:
+            ahead.append(start(c + 2))
         fresh = [
             jnp.sum(query * new_key[8 * j + c : 8 * j + c + 1], axis=1, keepdims=True)
             for j in range(2)

time: 102 us -> 99.9 us (0.979)
  Pallas kernels: 9.36 us -> 7.84 us
    pallas_call x1, Pallas kernels: 5.6 us -> 4.08 us  [attend(): call(attend_kernel, (jax.ShapeDtypeStruct((128, 768), BF16), jax.ShapeDty...]
where the time goes in v3:
time: 99.9 us; the launch traced here: 99.6 us
  blocking collectives  90.4 us (90%)
  Pallas kernels  7.84 us (8%)
  between operations  1.31 us (1%)
    all_to_all x1, blocking collectives, exchange(): lax.all_to_all(packed.reshape(64, 8, 896), ('p', 'i'), 0, 0, tiled=True)  31.3 us
    all_to_all x1, blocking collectives, exchange(): arrived = lax.all_to_all(finished, ('p', 'i'), 0, 0, tiled=True)  29.9 us
    all_to_all x1, blocking collectives, exchange(): arrived = lax.all_to_all(message, 'n', 0, 0, tiled=True)  16.9 us
    all_to_all x1, blocking collectives, exchange(): arrived = lax.all_to_all(partial, 'n', 0, 0, tiled=True)  12.4 us
    pallas_call x1, Pallas kernels, attend(): call(attend_kernel, (jax.ShapeDtypeStruct((128, 768), BF16), jax.ShapeDty...  4.08 us
    pallas_call x1, Pallas kernels, exchange(): call(project_kernel, (pltpu.VMEM((64, 128), F32), pltpu.VMEM((2, 64, 128)...  2.19 us

profile of v3, /device:TPU:1, one launch (start us, length us, event | category | flops | bytes accessed | tf_op | source)
XLA Modules:
  0.0 99.6 jit_solution(6802402345804842013)
XLA Ops:
  1.3 2.2 %project.1 = (f32[64,128]{1,0:T(8,128)S(1)}, f32[2,64,128]{2,1,0:T(8,128)S(1)}, f32[8,8,896]{2,1,0:T(8,128)S(1)}, bf16[125,768]{1,0:T(8,128)(2,1)S(1)}, bf16[125...) custom-call(s32[1]{0:T(128)S(6)} %copy.11.assign_ref, s32[1,2,64]{2,1,0:T(2,128)} %ids_ref.1, f32[768]{0:T(1024)} %gain_ref.1, ...), custom_call_target="tpu_custom_call" | custom-call | flops 268435456 | bytes 1048576 | tf_op jit(solution)/shard_map/project/pallas_call | solution.py:211
  3.5 12.4 %all_to_all.20.arrived_ref = f32[8,8,896]{2,1,0:T(8,128)S(1)} all-to-all(f32[8,8,896]{2,1,0:T(8,128)S(1)} %get-tuple-element.12), channel_id=1, replica_groups=mesh['p'=8,'i'=8,'n'=8] {'n'}, dimensions={0} | all-to-all | bytes 458752 | tf_op jit(solution)/shard_map/all_to_all | solution.py:228
  15.9 0.1 finish.1
  16.0 29.9 %all_to_all.21.arrived_ref = bf16[64,8,128]{2,1,0:T(8,128)(2,1)S(1)} all-to-all(bf16[64,8,128]{2,1,0:T(8,128)(2,1)S(1)} %finish.1), channel_id=1, replica_groups=mesh['p'=8,'i'=8,'n'=8] {'p','i'}, dimensions={0} | all-to-all | bytes 262144 | tf_op jit(solution)/shard_map/all_to_all | solution.py:232
  45.9 0.9 pack.1
  46.8 31.3 %all_to_all.22 = bf16[64,8,896]{2,1,0:T(8,128)(2,1)S(1)} all-to-all(bf16[64,8,896]{2,1,0:T(8,128)(2,1)S(1)} %bitcast.5), channel_id=1, replica_groups=mesh['p'=8,'i'=8,'n'=8] {'p','i'}, dimensions={0} | all-to-all | bytes 1835008 | tf_op jit(solution)/shard_map/all_to_all | solution.py:240
  78.0 0.6 unpack.1
  78.6 16.9 %all_to_all.23.arrived_ref = bf16[8,16,3968]{2,1,0:T(8,128)(2,1)S(1)} all-to-all(bf16[8,16,3968]{2,1,0:T(8,128)(2,1)S(1)} %get-tuple-element.19), channel_id=1, replica_groups=mesh['p'=8,'i'=8,'n'=8] {'n'}, dimensions={0} | all-to-all | bytes 2031616 | tf_op jit(solution)/shard_map/all_to_all | solution.py:247
  95.5 4.1 %attend.1 = (bf16[128,768]{1,0:T(8,128)(2,1)}, bf16[2,8,6144]{2,1,0:T(8,128)(2,1)}) custom-call(bf16[128,768]{1,0:T(8,128)(2,1)S(1)} %get-tuple-element.18.query_ref, bf16[8,16,3968]{2,1,0:T(8,128)(2,1)S(1)} %all_to_all.23.arrived_ref, bf16[8,768,256]{2,1,0:T(8,128)(2,1)} %bitcast.7), custom_call_target="tpu_custom_call" | custom-call | flops 1073741824 | bytes 1048576 | tf_op jit(solution)/shard_map/attend/pallas_call | solution.py:357

commit v4 on v3

--- a/solution.py
+++ b/solution.py
@@ -85,19 +85,18 @@
     lane8 = lax.broadcasted_iota(jnp.int32, (64, 128), 1)
     asked = total - 1.0 + jnp.where((lane8 & 4) != 0, 128.0, 0.0)
     asked = jnp.where(total > 0.5, asked, -1.0)
-    problem = assign_ref[...].astype(F32).reshape(1, 1)
-    req_ref[...] = jnp.where(lane8 >= 64, problem, asked)
-
-
-def project_kernel(assign_ref, ids_ref, gain_ref, far_hidden_ref, far_weight_ref, *refs):
-    req_ref, slot_ref, out_ref = refs[3:6]
-    far = (far_hidden_ref, far_weight_ref, *refs[0:3])
-    hidden_ref, weight_ref = refs[9:11]
-    near = (hidden_ref, weight_ref, *refs[6:9])
-    copies = [pltpu.make_async_copy(far[k], near[k], refs[11].at[k]) for k in range(5)]
+    req_ref[...] = jnp.where(lane8 >= 64, assign_ref[0].astype(F32), asked)
+
+
+def project_kernel(*refs):
+    far, (req_ref, slot_ref, out_ref), near = refs[1:8], refs[8:11], (*refs[14:18], *refs[11:14])
+    assign_ref, arrivals = refs[0], refs[18]
+    hidden_ref, weight_ref, gain_ref, ids_ref = near[0:4]
+    copies = [pltpu.make_async_copy(far[k], near[k], arrivals.at[k]) for k in range(7)]
     for copy in copies:
         copy.start()
     copies[0].wait()
+    copies[2].wait()
     hidden = hidden_ref[...].astype(F32)
     scaled = (hidden * gain_ref[...].reshape(1, -1)).astype(BF16)
     copies[1].wait()
@@ -111,8 +110,9 @@
             out_ref[k, :, 256 * m : 256 * m + 256] = proj[at : at + 8]
             tile = jnp.where(lane == m, squares[at : at + 8], tile)
         out_ref[k, :, 768:896] = tile
+    copies[3].wait()
     request(assign_ref, ids_ref, req_ref, slot_ref)
-    for copy in copies[2:]:
+    for copy in copies[4:]:
         copy.wait()
 
 
@@ -137,7 +137,9 @@
             out_ref[w] = jnp.where(row == 6, req_ref[w : w + 1, :], base).astype(BF16)
 
 
-def pack_kernel(arrived_ref, cross_ref, self_ref, kv_ref, out_ref, table_ref, new_ref):
+def pack_kernel(
+    arrived_ref, cross_ref, self_ref, kv_ref, out_ref, table_ref, new_ref, rows_ref
+):
     outer = lax.axis_index("p")
     narrow = lax.axis_index("n")
     rank = narrow >> 1
@@ -171,10 +173,17 @@
         info = jnp.sum(jnp.where(lane == want_extra, asked, 0.0), axis=1, keepdims=True)
         own = jnp.where(j_col < 6.0, info * 64.0 + outer_row + j_col, -1.0)
         new = jnp.where(j_col == 6.0, info, -1.0)
-        out_ref[at : at + 64, 0:768] = pick(onehot(lanes_table == row), table_ref[...]).astype(BF16)
-        out_ref[at : at + 64, 768:896] = (
-            pick(onehot(lanes_kv == own), arrived_ref[...].reshape(512, 128))
-            + pick(onehot(lanes_new == new), new_ref[...])
+        rows_ref[at : at + 64, 0:256] = onehot(lanes_table == row)
+        rows_ref[at : at + 64, 256:768] = onehot(lanes_kv == own)
+        rows_ref[at : at + 64, 768:896] = onehot(lanes_new == new)
+    for half in range(2):
+        at = 256 * half
+        out_ref[at : at + 256, 0:768] = pick(
+            rows_ref[at : at + 256, 0:256], table_ref[...]
+        ).astype(BF16)
+        out_ref[at : at + 256, 768:896] = (
+            pick(rows_ref[at : at + 256, 256:768], arrived_ref[...].reshape(512, 128))
+            + pick(rows_ref[at : at + 256, 768:896], new_ref[...])
         ).astype(BF16)
 
 
@@ -208,6 +217,7 @@
     enc_hidden, enc_gain, cross_weight, assign, token_ids, cross_table, self_table, kv_table
 ):
     tables = (cross_table, self_table, kv_table)
+    inputs = (enc_hidden, cross_weight, enc_gain, token_ids)
     asked, slot, partial, *tables = call(
         project_kernel,
         (
@@ -217,14 +227,13 @@
             *[pltpu.VMEM(x.shape, x.dtype) for x in tables],
         ),
         1 << 28,
-        in_specs=[vmem(), vmem(), vmem(), *[anywhere()] * 5],
+        in_specs=[smem(), *[anywhere()] * 7],
         scratch_shapes=[
-            pltpu.VMEM(enc_hidden.shape, BF16),
-            pltpu.VMEM(cross_weight.shape, BF16),
-            pltpu.SemaphoreType.DMA((5,)),
+            *[pltpu.VMEM(x.shape, x.dtype) for x in inputs],
+            pltpu.SemaphoreType.DMA((7,)),
         ],
         name="project",
-    )(assign, token_ids, enc_gain, enc_hidden, cross_weight, *tables)
+    )(assign, *inputs, *tables)
     arrived = lax.all_to_all(partial, "n", 0, 0, tiled=True)
     finished = call(finish_kernel, pltpu.VMEM((64, 8, 128), BF16), 1 << 20, name="finish")(
         held(arrived), held(asked)
@@ -234,7 +243,11 @@
         pack_kernel,
         pltpu.VMEM((512, 896), BF16),
         1 << 28,
-        scratch_shapes=[pltpu.VMEM((256, 768), BF16), pltpu.VMEM((128, 128), BF16)],
+        scratch_shapes=[
+            pltpu.VMEM((256, 768), BF16),
+            pltpu.VMEM((128, 128), BF16),
+            pltpu.VMEM((512, 896), BF16),
+        ],
         name="pack",
     )(held(arrived), *[held(x) for x in tables])
     arrived = lax.all_to_all(packed.reshape(64, 8, 896), ("p", "i"), 0, 0, tiled=True)

time: 99.9 us -> 99.2 us (level)
  no operation moved by 1% of the time
where the time goes in v4:
time: 99.2 us; the launch traced here: 98.9 us
  blocking collectives  90.4 us (91%)
  Pallas kernels  7.21 us (7%)
  between operations  1.31 us (1%)
    all_to_all x1, blocking collectives, exchange(): lax.all_to_all(packed.reshape(64, 8, 896), ('p', 'i'), 0, 0, tiled=True)  31.3 us
    all_to_all x1, blocking collectives, exchange(): arrived = lax.all_to_all(finished, ('p', 'i'), 0, 0, tiled=True)  29.9 us
    all_to_all x1, blocking collectives, exchange(): arrived = lax.all_to_all(message, 'n', 0, 0, tiled=True)  16.9 us
    all_to_all x1, blocking collectives, exchange(): arrived = lax.all_to_all(partial, 'n', 0, 0, tiled=True)  12.4 us
    pallas_call x1, Pallas kernels, attend(): call(attend_kernel, (jax.ShapeDtypeStruct((128, 768), BF16), jax.ShapeDty...  4.1 us

profile of v4, /device:TPU:1, one launch (start us, length us, event | category | flops | bytes accessed | tf_op | source)
XLA Modules:
  0.0 98.9 jit_solution(4237610871166275543)
XLA Ops:
  1.3 1.7 %project.1 = (f32[64,128]{1,0:T(8,128)S(1)}, f32[2,64,128]{2,1,0:T(8,128)S(1)}, f32[8,8,896]{2,1,0:T(8,128)S(1)}, bf16[125,768]{1,0:T(8,128)(2,1)S(1)}, bf16[125...) custom-call(s32[1]{0:T(128)S(6)} %copy.11.refs_0_, bf16[192,768]{1,0:T(8,128)(2,1)} %refs_1_.1, ...), custom_call_target="tpu_custom_call" | custom-call | flops 268435456 | bytes 1048576 | tf_op jit(solution)/shard_map/project/pallas_call | solution.py:221
  3.0 12.4 %all_to_all.20.arrived_ref = f32[8,8,896]{2,1,0:T(8,128)S(1)} all-to-all(f32[8,8,896]{2,1,0:T(8,128)S(1)} %get-tuple-element.12), channel_id=1, replica_groups=mesh['p'=8,'i'=8,'n'=8] {'n'}, dimensions={0} | all-to-all | bytes 458752 | tf_op jit(solution)/shard_map/all_to_all | solution.py:237
  15.4 0.1 finish.1
  15.5 29.9 %all_to_all.21.arrived_ref = bf16[64,8,128]{2,1,0:T(8,128)(2,1)S(1)} all-to-all(bf16[64,8,128]{2,1,0:T(8,128)(2,1)S(1)} %finish.1), channel_id=1, replica_groups=mesh['p'=8,'i'=8,'n'=8] {'p','i'}, dimensions={0} | all-to-all | bytes 262144 | tf_op jit(solution)/shard_map/all_to_all | solution.py:241
  45.4 0.7 pack.1
  46.1 31.3 %all_to_all.22 = bf16[64,8,896]{2,1,0:T(8,128)(2,1)S(1)} all-to-all(bf16[64,8,896]{2,1,0:T(8,128)(2,1)S(1)} %bitcast.5), channel_id=1, replica_groups=mesh['p'=8,'i'=8,'n'=8] {'p','i'}, dimensions={0} | all-to-all | bytes 1835008 | tf_op jit(solution)/shard_map/all_to_all | solution.py:253
  77.4 0.6 unpack.1
  78.0 16.9 %all_to_all.23.arrived_ref = bf16[8,16,3968]{2,1,0:T(8,128)(2,1)S(1)} all-to-all(bf16[8,16,3968]{2,1,0:T(8,128)(2,1)S(1)} %get-tuple-element.19), channel_id=1, replica_groups=mesh['p'=8,'i'=8,'n'=8] {'n'}, dimensions={0} | all-to-all | bytes 2031616 | tf_op jit(solution)/shard_map/all_to_all | solution.py:260
  94.8 4.1 %attend.1 = (bf16[128,768]{1,0:T(8,128)(2,1)}, bf16[2,8,6144]{2,1,0:T(8,128)(2,1)}) custom-call(bf16[128,768]{1,0:T(8,128)(2,1)S(1)} %get-tuple-element.18.query_ref, bf16[8,16,3968]{2,1,0:T(8,128)(2,1)S(1)} %all_to_all.23.arrived_ref, bf16[8,768,256]{2,1,0:T(8,128)(2,1)} %bitcast.7), custom_call_target="tpu_custom_call" | custom-call | flops 1073741824 | bytes 1048576 | tf_op jit(solution)/shard_map/attend/pallas_call | solution.py:370

commit v5 on v4

--- a/solution.py
+++ b/solution.py
@@ -191,19 +191,27 @@
     rank = (lax.axis_index("n") >> 1).astype(F32)
     lanes = iota((128, 512), 1)
     spread = jnp.concatenate([slot_ref[0], slot_ref[1]], axis=0)[:, 0:1]
-    cross_ref[...] = pick(onehot(lanes == spread), arrived_ref[:, 0:768]).astype(BF16)
     slot = jnp.concatenate(
         [slot_ref[t, 8 * k : 8 * k + 8] for k in range(PART) for t in range(2)], axis=0
     )[:, 0:1]
-    self_q = pick(onehot(lanes == slot + 4.0), arrived_ref[:, 0:768]).astype(BF16)
+    queries = pick(
+        jnp.concatenate([onehot(lanes == spread), onehot(lanes == slot + 4.0)], axis=0),
+        arrived_ref[:, 0:768],
+    ).astype(BF16)
+    cross_ref[...] = queries[0:128]
+    self_q = queries[128:256]
     own_rank = slot - 8.0 * jnp.floor(slot * 0.125)
     piece = jnp.where(own_rank == rank, slot - own_rank + 6.0, -1.0)
-    new = pick(onehot(lanes == piece), arrived_ref[:, 768:896]).astype(BF16)
     row = lax.broadcasted_iota(jnp.int32, (192, 512), 0)
     source = (row & 63) * 8 + (row >> 6)
     column = lax.broadcasted_iota(jnp.int32, (192, 512), 1)
-    keys = pick(onehot(column == source), arrived_ref[:, 768:896]).astype(BF16)
-    values = pick(onehot(column == source + 3), arrived_ref[:, 768:896]).astype(BF16)
+    beside = pick(
+        jnp.concatenate(
+            [onehot(lanes == piece), onehot(column == source), onehot(column == source + 3)], axis=0
+        ),
+        arrived_ref[:, 768:896],
+    ).astype(BF16)
+    new, keys, values = beside[0:128], beside[128:320], beside[320:512]
     for k in range(PART):
         out_ref[k, :, 0:768] = self_q[16 * k : 16 * k + 16]
         out_ref[k, :, 768:896] = new[16 * k : 16 * k + 16]

time: 99.2 us -> 99.2 us (level)
  no operation moved by 1% of the time
where the time goes in v5:
time: 99.2 us; the launch traced here: 98.9 us
  blocking collectives  90.4 us (91%)
  Pallas kernels  7.21 us (7%)
  between operations  1.31 us (1%)
    all_to_all x1, blocking collectives, exchange(): lax.all_to_all(packed.reshape(64, 8, 896), ('p', 'i'), 0, 0, tiled=True)  31.3 us
    all_to_all x1, blocking collectives, exchange(): arrived = lax.all_to_all(finished, ('p', 'i'), 0, 0, tiled=True)  29.9 us
    all_to_all x1, blocking collectives, exchange(): arrived = lax.all_to_all(message, 'n', 0, 0, tiled=True)  16.9 us
    all_to_all x1, blocking collectives, exchange(): arrived = lax.all_to_all(partial, 'n', 0, 0, tiled=True)  12.4 us
    pallas_call x1, Pallas kernels, attend(): call(attend_kernel, (jax.ShapeDtypeStruct((128, 768), BF16), jax.ShapeDty...  4.1 us

profile of v5, /device:TPU:1, one launch (start us, length us, event | category | flops | bytes accessed | tf_op | source)
XLA Modules:
  0.0 98.9 jit_solution(15485132495252465506)
XLA Ops:
  1.3 1.7 %project.1 = (f32[64,128]{1,0:T(8,128)S(1)}, f32[2,64,128]{2,1,0:T(8,128)S(1)}, f32[8,8,896]{2,1,0:T(8,128)S(1)}, bf16[125,768]{1,0:T(8,128)(2,1)S(1)}, bf16[125...) custom-call(s32[1]{0:T(128)S(6)} %copy.11.refs_0_, bf16[192,768]{1,0:T(8,128)(2,1)} %refs_1_.1, ...), custom_call_target="tpu_custom_call" | custom-call | flops 268435456 | bytes 1048576 | tf_op jit(solution)/shard_map/project/pallas_call | solution.py:229
  3.0 12.4 %all_to_all.20.arrived_ref = f32[8,8,896]{2,1,0:T(8,128)S(1)} all-to-all(f32[8,8,896]{2,1,0:T(8,128)S(1)} %get-tuple-element.12), channel_id=1, replica_groups=mesh['p'=8,'i'=8,'n'=8] {'n'}, dimensions={0} | all-to-all | bytes 458752 | tf_op jit(solution)/shard_map/all_to_all | solution.py:245
  15.4 0.1 finish.1
  15.5 29.9 %all_to_all.21.arrived_ref = bf16[64,8,128]{2,1,0:T(8,128)(2,1)S(1)} all-to-all(bf16[64,8,128]{2,1,0:T(8,128)(2,1)S(1)} %finish.1), channel_id=1, replica_groups=mesh['p'=8,'i'=8,'n'=8] {'p','i'}, dimensions={0} | all-to-all | bytes 262144 | tf_op jit(solution)/shard_map/all_to_all | solution.py:249
  45.4 0.7 pack.1
  46.1 31.3 %all_to_all.22 = bf16[64,8,896]{2,1,0:T(8,128)(2,1)S(1)} all-to-all(bf16[64,8,896]{2,1,0:T(8,128)(2,1)S(1)} %bitcast.5), channel_id=1, replica_groups=mesh['p'=8,'i'=8,'n'=8] {'p','i'}, dimensions={0} | all-to-all | bytes 1835008 | tf_op jit(solution)/shard_map/all_to_all | solution.py:261
  77.4 0.6 unpack.1
  78.0 16.9 %all_to_all.23.arrived_ref = bf16[8,16,3968]{2,1,0:T(8,128)(2,1)S(1)} all-to-all(bf16[8,16,3968]{2,1,0:T(8,128)(2,1)S(1)} %get-tuple-element.19), channel_id=1, replica_groups=mesh['p'=8,'i'=8,'n'=8] {'n'}, dimensions={0} | all-to-all | bytes 2031616 | tf_op jit(solution)/shard_map/all_to_all | solution.py:268
  94.8 4.1 %attend.1 = (bf16[128,768]{1,0:T(8,128)(2,1)}, bf16[2,8,6144]{2,1,0:T(8,128)(2,1)}) custom-call(bf16[128,768]{1,0:T(8,128)(2,1)S(1)} %get-tuple-element.18.query_ref, bf16[8,16,3968]{2,1,0:T(8,128)(2,1)S(1)} %all_to_all.23.arrived_ref, bf16[8,768,256]{2,1,0:T(8,128)(2,1)} %bitcast.7), custom_call_target="tpu_custom_call" | custom-call | flops 1073741824 | bytes 1048576 | tf_op jit(solution)/shard_map/attend/pallas_call | solution.py:378
